TPU v7x, 256 devices: a whole 4x4x8 slice. The times are simulated.
256 devices in a mesh: ctx: 64 (over x, z, core), tp: 4 (over y).
Axes of the slice: x: 4, y: 4, z: 8, core: 2. Of those that a mesh axis runs over, the one named last changes fastest.
Arguments:
- queries: bfloat16 [12288, 4096], P(('ctx', 'tp')), may hold values from -64 to 64
- keys: bfloat16 [12288, 512], P(('ctx', 'tp')), may hold values from -6 to 6
- values: bfloat16 [12288, 512], P(('ctx', 'tp')), may hold values from -6 to 6
- block_order: int32 [128], replicated, may hold values from 0 to 127, as said below
Outputs:
- attended: bfloat16 [12288, 4096], P(('ctx', 'tp'))
Inputs may be any that keep to these rules, and one draw needn't show every extreme that they name: block_order is a permutation of the 128 blocks in which slots 2 c and 2 c + 1 hold blocks p and 127 - p for some p, in either order.
All inputs are finite; a program needn't handle non-finite values.
Results may differ from a plain program's by a relative error of at most 0.0055.
Values may be sent and summed in bfloat16 or wider, within the bound.
No kernel may reach another device: no remote copies, remote signals or barrier semaphores. Data moves between devices by JAX's collectives and lax.ppermute only.
A program may use at most 64 MiB of HBM per device.

v0:
```python
import functools
import math

import jax
import jax.numpy as jnp
import numpy as np
from jax import lax
from jax.experimental import pallas as pl
from jax.experimental.pallas import tpu as pltpu
from jax.sharding import Mesh, PartitionSpec as P


QUERY_HEAD_COUNT = 32
KEY_VALUE_HEADS = 4
HEAD = 128
GROUP = QUERY_HEAD_COUNT // KEY_VALUE_HEADS
BLOCK = 96
LANES = GROUP * BLOCK
TILE = 8
WIDE = 256
NEG = -1e30
LOG2_SCALE = HEAD ** -0.5 * math.log2(math.e)
TOO_LARGE = 2.0**60
ROWS = HEAD + 8
NX, NZ = 4, 8


def shift(n, k):
    return [(i, (i + k) % n) for i in range(n)]


def attend_kernel(counts, first, sides, *refs):
    cnt, seen, idx, kpos, qpos = refs[:5]
    at = 5 + len(sides)
    queries = refs[5:at]
    pieces = refs[at : at + len(counts)]
    at += len(counts)
    if not first:
        before = refs[at : at + len(sides)]
        at += len(sides)
    outs = refs[at : at + len(sides)]
    kv, q_turned, work, sems = refs[at + len(sides) :]
    copies, row = [], 0
    for i, n in enumerate(counts):
        copy = pltpu.make_async_copy(pieces[i], kv.at[pl.ds(row * BLOCK, n * BLOCK)], sems.at[i])
        copy.start()
        copies.append(copy)
        row += n
    for copy in copies:
        copy.wait()

    def fetch(qb, place, width):
        offs = [pl.multiple_of(idx[qb, place + j] * BLOCK, BLOCK) for j in range(width)]
        keys = jnp.concatenate([kv[pl.ds(f, BLOCK), 0:HEAD] for f in offs], 0)
        return keys, jnp.concatenate([kv[pl.ds(f, BLOCK), HEAD : 2 * HEAD] for f in offs], 0).T

    def pipelined(keys, mask, soften, weigh):
        chunks = LANES // WIDE

        def logits(c):
            s = jnp.dot(keys, q_turned[:, c * WIDE : (c + 1) * WIDE], preferred_element_type=jnp.float32)
            return mask(c, s)

        s, held = logits(0), None
        for c in range(chunks):
            following = logits(c + 1) if c + 1 < chunks else None
            now = soften(slice(c * WIDE, (c + 1) * WIDE), s)
            if held is not None:
                weigh(*held)
            held, s = now, following
        weigh(*held)

    def careful(qb, place):
        keys, vals = fetch(qb, place, 2)
        inner = lax.broadcasted_iota(jnp.int32, (BLOCK, 1), 0)
        kp = jnp.concatenate([inner + kpos[qb, place + j] * BLOCK for j in range(2)], 0)

        def mask(c, s):
            lane = lax.broadcasted_iota(jnp.int32, (1, WIDE), 1) + c * WIDE
            return jnp.where(kp <= lane % BLOCK + qpos[qb] * BLOCK, s, NEG)

        def soften(sl, s):
            top = work[HEAD : HEAD + 1, sl]
            new = jnp.maximum(top, jnp.max(s, 0, keepdims=True))
            p = jnp.exp2((s - new) * LOG2_SCALE)
            decay = jnp.exp2((top - new) * LOG2_SCALE)
            work[HEAD : HEAD + 1, sl] = new
            work[HEAD + 1 : HEAD + 2, sl] = work[HEAD + 1 : HEAD + 2, sl] * decay + jnp.sum(p, 0, keepdims=True)
            return sl, p.astype(jnp.bfloat16), decay

        def weigh(sl, p, decay):
            work[0:HEAD, sl] = work[0:HEAD, sl] * decay + jnp.dot(vals, p, preferred_element_type=jnp.float32)

        pipelined(keys, mask, soften, weigh)

    def quick(qb, place, width, left):
        keys, vals = fetch(qb, place, width)
        cut = (width - 1) * BLOCK

        def mask(c, s):
            if left is None:
                return s
            return jnp.concatenate([s[:cut], s[cut:] + jnp.where(left == width, 0.0, NEG)], 0)

        def soften(sl, s):
            p = jnp.exp2((s - work[HEAD : HEAD + 1, sl]) * LOG2_SCALE)
            work[HEAD + 1 : HEAD + 2, sl] += jnp.sum(p, 0, keepdims=True)
            return sl, p.astype(jnp.bfloat16)

        def weigh(sl, p):
            work[0:HEAD, sl] += jnp.dot(vals, p, preferred_element_type=jnp.float32)

        pipelined(keys, mask, soften, weigh)

    def query_block(b, carry):
        qb = 2 * sides[0] + b
        n = cnt[qb]
        lead = jnp.where((seen[qb] == 0) | (kpos[qb, 0] == qpos[qb]), jnp.minimum(n, 1), 0)
        full = lax.div(jnp.maximum(n - 2 * lead, 0), TILE)
        at = 2 * lead + full * TILE
        left = n - at

        def load():
            if first:
                work[0:HEAD] = jnp.zeros((HEAD, LANES), jnp.float32)
                work[HEAD : HEAD + 1] = jnp.full((1, LANES), NEG, jnp.float32)
                work[HEAD + 1 : ROWS] = jnp.zeros((ROWS - HEAD - 1, LANES), jnp.float32)
            else:
                for i in range(len(sides)):

                    @pl.when(b // 2 == i)
                    def _():
                        work[...] = before[i][b % 2]

        load()
        for i in range(len(sides)):

            @pl.when(b // 2 == i)
            def _():
                start = pl.multiple_of(b % 2 * BLOCK, BLOCK)
                heads = [queries[i][pl.ds(start, BLOCK), h * HEAD : (h + 1) * HEAD] for h in range(GROUP)]
                q_turned[...] = jnp.concatenate(heads, 0).T

        def slow(t, carry):
            careful(qb, t * 2)
            return carry

        def fast(t, carry):
            quick(qb, 2 * lead + t * TILE, TILE, None)
            return carry

        lax.fori_loop(0, lead, slow, 0)
        lax.fori_loop(0, full, fast, 0)
        for width in range(2, TILE + 1, 2):

            @pl.when((left == width) | (left == width - 1))
            def _():
                quick(qb, at, width, left)

        fine = jnp.max(jnp.where(work[HEAD + 1 : HEAD + 2] < TOO_LARGE, 0.0, 1.0)) == 0.0

        @pl.when(jnp.logical_not(fine))
        def _():
            load()
            lax.fori_loop(0, lax.div(n + 1, 2), slow, 0)

        for i in range(len(sides)):

            @pl.when(b // 2 == i)
            def _():
                outs[i][b % 2] = work[...]

        return carry

    lax.fori_loop(0, 2 * len(sides), query_block, 0)


def attend(tables, qpos, queries, pieces, state, sides=(0, 1)):
    counts = [p.shape[0] // BLOCK for p in pieces]
    total = sum(counts)
    first = state is None
    smem = pl.BlockSpec(memory_space=pltpu.SMEM)
    vmem = pl.BlockSpec(memory_space=pltpu.VMEM)
    anywhere = pl.BlockSpec(memory_space=pl.ANY)
    held = [] if first else [state[i] for i in sides]
    shape = jax.ShapeDtypeStruct((2, ROWS, LANES), jnp.float32)
    return pl.pallas_call(
        functools.partial(attend_kernel, counts, first, sides),
        out_shape=(shape,) * len(sides),
        in_specs=[smem] * 5 + [vmem] * len(sides) + [anywhere] * len(pieces) + [vmem] * len(held),
        out_specs=(vmem,) * len(sides),
        scratch_shapes=[
            pltpu.VMEM((total * BLOCK, 2 * HEAD), jnp.bfloat16),
            pltpu.VMEM((HEAD, LANES), jnp.bfloat16),
            pltpu.VMEM((ROWS, LANES), jnp.float32),
            pltpu.SemaphoreType.DMA((len(pieces),)),
        ],
        compiler_params=pltpu.CompilerParams(vmem_limit_bytes=32 * 1024 * 1024),
        cost_estimate=pl.CostEstimate(
            flops=total * len(sides) * LANES * BLOCK * HEAD * 4,
            bytes_accessed=total * BLOCK * 4 * HEAD + 4 * ROWS * LANES * 4,
            transcendentals=total * len(sides) * LANES * BLOCK,
        ),
        name="attend",
    )(*tables, qpos, *[queries[i] for i in sides], *pieces, *held)


def tables_of(qblk, kblk):
    nb = kblk.shape[1]
    here = jnp.arange(nb, dtype=jnp.int32)
    k, q = kblk[:, None, :], qblk[None, :, None]
    rank = jnp.where(k <= q, jnp.where(k == q, -1, here), 2 * nb + here)
    place = jnp.sum(rank[:, :, None, :] < rank[:, :, :, None], 3)
    hit = place[:, :, :, None] == here
    idx = jnp.sum(jnp.where(hit, here[:, None], 0), 2).astype(jnp.int32)
    kpos = jnp.sum(jnp.where(hit, k[:, :, :, None], 0), 2).astype(jnp.int32)
    cnt = jnp.sum(k <= q, 2).astype(jnp.int32)
    return cnt, jnp.cumsum(cnt, 0) - cnt, idx, kpos


def merge_kernel(mine, theirs, out):
    for b in range(2):
        m1, m2 = mine[b, HEAD : HEAD + 1], theirs[b, HEAD : HEAD + 1]
        top = jnp.maximum(m1, m2)
        w1 = jnp.exp2((m1 - top) * LOG2_SCALE)
        w2 = jnp.exp2((m2 - top) * LOG2_SCALE)
        denom = mine[b, HEAD + 1 : HEAD + 2] * w1 + theirs[b, HEAD + 1 : HEAD + 2] * w2
        o = (mine[b, 0:HEAD] * w1 + theirs[b, 0:HEAD] * w2) / denom
        rows = o.T.astype(jnp.bfloat16)
        for h in range(GROUP):
            out[b * BLOCK : (b + 1) * BLOCK, h * HEAD : (h + 1) * HEAD] = rows[h * BLOCK : (h + 1) * BLOCK]


def merge(mine, theirs):
    return pl.pallas_call(
        merge_kernel,
        out_shape=jax.ShapeDtypeStruct((2 * BLOCK, GROUP * HEAD), jnp.bfloat16),
        compiler_params=pltpu.CompilerParams(vmem_limit_bytes=16 * 1024 * 1024),
        name="merge",
    )(mine, theirs)


def lookup(block_order, index):
    table = jnp.arange(block_order.shape[0], dtype=jnp.int32)
    return jnp.sum(jnp.where(index[:, None] == table[None, :], block_order[None, :], 0), axis=1)


def attention(queries, keys, values, block_order):
    rows = queries.shape[0]
    x, z, c = lax.axis_index("x"), lax.axis_index("z"), lax.axis_index("c")
    pair = jnp.concatenate([keys.reshape(rows, 4, HEAD), values.reshape(rows, 4, HEAD)], 2).transpose(1, 0, 2)
    spread = jnp.broadcast_to(pair[None], (NX, 4, rows, 2 * HEAD)).reshape(NX * 4, rows, 2 * HEAD)
    line = lax.all_to_all(spread, ("x", "tp"), split_axis=0, concat_axis=0, tiled=True).reshape(-1, 2 * HEAD)

    q_own = lax.all_to_all(queries, "tp", split_axis=1, concat_axis=0, tiled=True)
    q_other = lax.ppermute(q_own, "c", shift(2, 1))

    ctx = (x * NZ + z) * 2
    own = np.asarray([1, 1, 0, 0], np.int32)
    core = own * c + (1 - own) * (1 - c)
    qpos = lookup(block_order, 2 * (ctx + core) + np.asarray([0, 1, 0, 1], np.int32))

    offsets = [(0, -1, 1), (-2, 2), (-3, 3), (NZ // 2,)]
    most = 2 * NX * max(len(o) for o in offsets)
    dz, dx, slot, real = (np.zeros((len(offsets), most), np.int32) for _ in range(4))
    for i, group in enumerate(offsets):
        for j, (o, xs, sl) in enumerate((o, xs, sl) for o in group for xs in range(NX) for sl in range(2)):
            dz[i, j], dx[i, j], slot[i, j], real[i, j] = o, xs, sl, 1
    stored = lookup(block_order, (2 * ((dx * NZ + (z + dz) % NZ) * 2 + c) + slot).reshape(-1)).reshape(dz.shape)
    tables = tables_of(qpos, jnp.where(real == 1, stored, 1 << 20))

    up, down = lax.ppermute(line, "z", shift(NZ, 1)), lax.ppermute(line, "z", shift(NZ, -1))
    pieces, state = [line, up, down], None
    for i in range(len(offsets)):
        if i < len(offsets) - 2:
            up, down = lax.ppermute(up, "z", shift(NZ, 1)), lax.ppermute(down, "z", shift(NZ, -1))
        elif i == len(offsets) - 2:
            half = line.shape[0] // 2
            up, down = lax.ppermute(up[:half], "z", shift(NZ, 1)), lax.ppermute(down[half:], "z", shift(NZ, -1))
        part = [t[i] for t in tables]
        if i < len(offsets) - 1:
            state = attend(part, qpos, (q_own, q_other), pieces, state)
            up, down, state = lax.optimization_barrier((up, down, state))
            pieces = [up, down]
    (sent,) = attend(part, qpos, (q_own, q_other), pieces, state, (1,))
    theirs = lax.ppermute(sent, "c", shift(2, 1))
    (mine,) = attend(part, qpos, (q_own, q_other), pieces, state, (0,))
    result = merge(mine, theirs)
    return lax.all_to_all(result, "tp", split_axis=0, concat_axis=1, tiled=True)


def solution(mesh):
    cut = Mesh(mesh.devices.reshape(NX, NZ, 2, 4), ("x", "z", "c", "tp"))
    placed = P(("x", "z", "c", "tp"), None)
    return jax.shard_map(attention, mesh=cut, in_specs=(placed, placed, placed, P()), out_specs=placed, check_vma=False)
```

profile of v0, /device:TPU:1, one launch (start us, length us, event | category | flops | bytes accessed | tf_op | source)
XLA Modules:
  0.0 86.3 jit_solution(17346872620203190990)
XLA Ops:
  0.0 0.0 copy-start.1
  0.0 0.8 reshape.44
  0.8 0.0 copy-done.1
  0.9 0.8 broadcast_in_dim.91
  1.7 0.0 copy-start.4
  1.7 0.0 copy-start
  1.7 7.7 %all-to-all-start.1 = ((bf16[16,48,256]{2,1,0:T(8,128)(2,1)}), bf16[16,48,256]{2,1,0:T(8,128)(2,1)S(1)}, u32[]{:S(2)}, u32[]{:S(2)}) async-start(bf16[16,48,256]{2,1,0:T(8,128)(2,1)} %bitcast.7), calls=%async_computation.1 | async-start | bytes 786432 | tf_op jit(solution)/shard_map/all_to_all | solution.py:253
  9.4 0.0 copy-start.3
  9.4 0.0 copy-start.2
  9.5 0.0 copy-done.4
  9.5 0.6 copy-done.3
  10.1 0.0 copy-done.2
  10.1 0.0 copy-start.8
  10.2 0.1 eq.60
  10.2 0.6 copy-done.8
  10.8 0.0 copy-start.9
  10.8 0.2 select_reduce_fusion.2
  11.0 0.5 copy-done.9
  11.5 0.1 reshape.50
  11.6 0.0 copy-done
  11.6 0.8 copy.21
  12.3 0.0 copy-start.5
  12.3 0.0 copy-start.6
  12.3 0.0 copy-start.7
  12.3 0.6 copy-done.5
  13.0 0.0 copy-done.6
  13.0 0.0 copy-done.7
  13.0 0.2 select_reduce_fusion.3.refs_4_
  13.2 4.5 %all-to-all-done.1 = bf16[16,48,256]{2,1,0:T(8,128)(2,1)S(1)} async-done(((bf16[16,48,256]{2,1,0:T(8,128)(2,1)}), bf16[16,48,256]{2,1,0:T(8,128)(2,1)S(1)}, u32[]{:S(2)}, u32[]{:S(2)}) %all-to-all-start.1) | async-done | bytes 393248 | tf_op jit(solution)/shard_map/all_to_all | solution.py:253
  17.7 3.5 %all-to-all-start = ((bf16[48,4,1024]{2,0,1:T(8,128)(2,1)}), bf16[48,4,1024]{2,0,1:T(8,128)(2,1)S(1)}, u32[]{:S(2)}, u32[]{:S(2)}) async-start(bf16[48,4,1024]{2,0,1:T(8,128)(2,1)} %bitcast.46), calls=%async_computation | async-start | bytes 786432 | tf_op jit(solution)/shard_map/all_to_all | solution.py:255
  21.2 0.2 compare_select_fusion
  21.4 5.7 %collective-permute-start.2 = (bf16[768,256]{1,0:T(8,128)(2,1)S(1)}, bf16[768,256]{1,0:T(8,128)(2,1)S(1)}, u32[]{:S(2)}, u32[]{:S(2)}) collective-permute-start(bf16[768,256]{1,0:T(8,128)(2,1)S(1)} %bitcast.53), channel_id=1, source_target_pairs={{0,56},{8,0},{16,8},{24,16},{32,24},{40,32},{48,40},{56,48},{1,57}... | collective-permute-start | bytes 1179656 | tf_op jit(solution)/shard_map/ppermute | solution.py:272
  27.0 0.0 collective-permute-start
  27.0 0.5 convert_reduce_fusion
  27.5 0.2 select_reduce_fusion
  27.7 0.0 all-to-all-done
  27.7 3.3 %collective-permute-start.4 = (bf16[192,1024]{1,0:T(8,128)(2,1)S(1)}, bf16[192,1024]{1,0:T(8,128)(2,1)S(1)}, u32[]{:S(2)}, u32[]{:S(2)}) collective-permute-start(bf16[192,1024]{1,0:T(8,128)(2,1)S(1)} %bitcast.47), channel_id=1, source_target_pairs={{0,4},{4,0},{1,5},{5,1},{2,6},{6,2},{3,7},{7,3},{8,12},{12,8},{9,1... | collective-permute-start | bytes 1179656 | tf_op jit(solution)/shard_map/ppermute | solution.py:256
  31.0 2.0 %collective-permute-done.2.refs_9_ = bf16[768,256]{1,0:T(8,128)(2,1)S(1)} collective-permute-done((bf16[768,256]{1,0:T(8,128)(2,1)S(1)}, bf16[768,256]{1,0:T(8,128)(2,1)S(1)}, u32[]{:S(2)}, u32[]{:S(2)}) %collective-permute-start.2) | collective-permute-done | bytes 393248 | tf_op jit(solution)/shard_map/ppermute | solution.py:272
  33.0 3.6 %collective-permute-start.3 = (bf16[768,256]{1,0:T(8,128)(2,1)S(1)}, bf16[768,256]{1,0:T(8,128)(2,1)S(1)}, u32[]{:S(2)}, u32[]{:S(2)}) collective-permute-start(bf16[768,256]{1,0:T(8,128)(2,1)S(1)} %collective-permute-done.2.refs_9_), channel_id=1, source_target_pairs={{0,56},{8,0},{16,8},{24,16},{32,24},{40,32},{48,40},{56,48},{1,57}... | collective-permute-start | bytes 1179656 | tf_op jit(solution)/shard_map/ppermute | solution.py:276
  36.6 0.0 collective-permute-done.refs_8_
  36.6 0.0 collective-permute-start.1
  36.6 0.0 collective-permute-done.4.refs_6_.refs_5_
  36.6 8.6 %attend.5 = (f32[2,136,768]{2,1,0:T(8,128)S(1)}, f32[2,136,768]{2,1,0:T(8,128)S(1)}) custom-call(s32[4]{0:T(128)S(1)} %get-tuple-element.66.refs_0_, s32[4]{0:T(128)S(1)} %get-tuple-element.55.refs_1_, s32[4,24]{1,0:T(4,128)S(1)} %get-tuple-element.62.refs_2_, s32[4,24]{1,0:T(4,128)S(1)} %get-tuple-element.45.refs_3_, s32[4]{0:T(128)S(1)} %select_reduce_fusion.3.refs_4_, ...), custom_call_target="tpu_custom_call" | custom-call | flops 1811939328 | bytes 2850816 | tf_op jit(solution)/shard_map/attend/pallas_call | solution.py:187
  45.3 0.0 collective-permute-done.3.refs_8_
  45.3 0.0 collective-permute-done.1.refs_7_
  45.3 0.1 collective-permute-start.5
  45.4 3.1 %collective-permute-start.6 = (bf16[768,256]{1,0:T(8,128)(2,1)S(1)}, bf16[768,256]{1,0:T(8,128)(2,1)S(1)}, u32[]{:S(2)}, u32[]{:S(2)}) collective-permute-start(bf16[768,256]{1,0:T(8,128)(2,1)S(1)} %collective-permute-done.3.refs_8_), channel_id=1, source_target_pairs={{0,56},{8,0},{16,8},{24,16},{32,24},{40,32},{48,40},{56,48},{1,57}... | collective-permute-start | bytes 1179656 | tf_op jit(solution)/shard_map/ppermute | solution.py:276
  48.4 5.3 %attend.6 = (f32[2,136,768]{2,1,0:T(8,128)S(1)}, f32[2,136,768]{2,1,0:T(8,128)S(1)}) custom-call(s32[4]{0:T(128)S(1)} %get-tuple-element.67.refs_0_, s32[4]{0:T(128)S(1)} %get-tuple-element.54.refs_1_, s32[4,24]{1,0:T(4,128)S(1)} %get-tuple-element.63.refs_2_, s32[4,24]{1,0:T(4,128)S(1)} %get-tuple-element.44.refs_3_, s32[4]{0:T(128)S(1)} %select_reduce_fusion.3.refs_4_, ...), custom_call_target="tpu_custom_call" | custom-call | flops 1207959552 | bytes 2457600 | tf_op jit(solution)/shard_map/attend/pallas_call | solution.py:187
  53.7 0.0 collective-permute-done.5.refs_7_
  53.8 0.0 collective-permute-done.6.refs_8_
  53.8 0.1 collective-permute-start.7
  53.9 2.7 %collective-permute-start.8 = (bf16[384,256]{1,0:T(8,128)(2,1)S(1)}, bf16[384,256]{1,0:T(8,128)(2,1)S(1)}, u32[]{:S(2)}, u32[]{:S(2)}) collective-permute-start(bf16[384,256]{1,0:T(8,128)(2,1)S(1)} %slice.67), channel_id=1, source_target_pairs={{0,56},{8,0},{16,8},{24,16},{32,24},{40,32},{48,40},{56,48},{1,57}... | collective-permute-start | bytes 589832 | tf_op jit(solution)/shard_map/ppermute | solution.py:279
  56.6 5.3 %attend.7 = (f32[2,136,768]{2,1,0:T(8,128)S(1)}, f32[2,136,768]{2,1,0:T(8,128)S(1)}) custom-call(s32[4]{0:T(128)S(1)} %get-tuple-element.68.refs_0_, s32[4]{0:T(128)S(1)} %get-tuple-element.53.refs_1_, s32[4,24]{1,0:T(4,128)S(1)} %get-tuple-element.64.refs_2_, s32[4,24]{1,0:T(4,128)S(1)} %get-tuple-element.43.refs_3_, s32[4]{0:T(128)S(1)} %select_reduce_fusion.3.refs_4_, ...), custom_call_target="tpu_custom_call" | custom-call | flops 1207959552 | bytes 2457600 | tf_op jit(solution)/shard_map/attend/pallas_call | solution.py:187
  61.9 0.0 collective-permute-done.7.refs_6_
  61.9 0.0 collective-permute-done.8.refs_7_
  61.9 2.5 %attend.9 = f32[2,136,768]{2,1,0:T(8,128)S(1)} custom-call(s32[4]{0:T(128)S(1)} %get-tuple-element.65.refs_0_, s32[4]{0:T(128)S(1)} %get-tuple-element.56.refs_1_, s32[4,24]{1,0:T(4,128)S(1)} %get-tuple-element.61.refs_2_, s32[4,24]{1,0:T(4,128)S(1)} %get-tuple-element.46.refs_3_, s32[4]{0:T(128)S(1)} %select_reduce_fusion.3.refs_4_, ...), custom_call_target="tpu_custom_call" | custom-call | flops 301989888 | bytes 2064384 | tf_op jit(solution)/shard_map/attend/pallas_call | solution.py:187
  64.4 5.9 %collective-permute-start.9 = (f32[2,136,768]{2,1,0:T(8,128)S(1)}, f32[2,136,768]{2,1,0:T(8,128)S(1)}, u32[]{:S(2)}, u32[]{:S(2)}) collective-permute-start(f32[2,136,768]{2,1,0:T(8,128)S(1)} %attend.9), channel_id=1, source_target_pairs={{0,4},{4,0},{1,5},{5,1},{2,6},{6,2},{3,7},{7,3},{8,12},{12,8},{9,1... | collective-permute-start | bytes 2506760 | tf_op jit(solution)/shard_map/ppermute | solution.py:286
  70.4 2.5 %attend.8.mine = f32[2,136,768]{2,1,0:T(8,128)S(1)} custom-call(s32[4]{0:T(128)S(1)} %get-tuple-element.65.refs_0_, s32[4]{0:T(128)S(1)} %get-tuple-element.56.refs_1_, s32[4,24]{1,0:T(4,128)S(1)} %get-tuple-element.61.refs_2_, s32[4,24]{1,0:T(4,128)S(1)} %get-tuple-element.46.refs_3_, s32[4]{0:T(128)S(1)} %select_reduce_fusion.3.refs_4_, ...), custom_call_target="tpu_custom_call" | custom-call | flops 301989888 | bytes 2064384 | tf_op jit(solution)/shard_map/attend/pallas_call | solution.py:187
  72.9 0.0 collective-permute-done.9.theirs
  72.9 0.2 merge.1
  73.2 12.3 %all_to_all.43 = bf16[4,48,1024]{2,1,0:T(8,128)(2,1)S(1)} all-to-all(bf16[4,48,1024]{2,1,0:T(8,128)(2,1)S(1)} %bitcast.52), channel_id=1, replica_groups=mesh['x'=4,'z'=8,'c'=2,'tp'=4] {'tp'}, dimensions={0} | all-to-all | bytes 786432 | tf_op jit(solution)/shard_map/all_to_all | solution.py:289
  85.5 0.8 copy.19
  (13 shorter events, 0.2 us)
Async XLA Ops:
  0.0 0.8 copy-start.1
  1.7 7.8 %copy-start.4 = (s32[4,24]{1,0:T(4,128)S(1)}, s32[4,24]{1,0:T(4,128)}, u32[]{:S(2)}) copy-start(s32[4,24]{1,0:T(4,128)} %constant.63.clone) | copy-start | bytes 1156
  1.7 9.8 %copy-start = (bf16[48,4096]{1,0:T(8,128)(2,1)S(1)}, bf16[48,4096]{1,0:T(8,128)(2,1)}, u32[]{:S(2)}) copy-start(bf16[48,4096]{1,0:T(8,128)(2,1)} %param.11) | copy-start | bytes 1179652
  1.7 16.0 %all-to-all-start.1 = ((bf16[16,48,256]{2,1,0:T(8,128)(2,1)}), bf16[16,48,256]{2,1,0:T(8,128)(2,1)S(1)}, u32[]{:S(2)}, u32[]{:S(2)}) async-start(bf16[16,48,256]{2,1,0:T(8,128)(2,1)} %bitcast.7), calls=%async_computation.1 | async-start | bytes 786432 | tf_op jit(solution)/shard_map/all_to_all | solution.py:253
  9.4 0.7 copy-start.3
  9.4 0.7 copy-start.2
  10.1 0.7 copy-start.8
  10.8 0.7 copy-start.9
  12.3 0.7 copy-start.5
  12.3 0.7 copy-start.6
  12.3 0.7 copy-start.7
  17.7 10.0 %all-to-all-start = ((bf16[48,4,1024]{2,0,1:T(8,128)(2,1)}), bf16[48,4,1024]{2,0,1:T(8,128)(2,1)S(1)}, u32[]{:S(2)}, u32[]{:S(2)}) async-start(bf16[48,4,1024]{2,0,1:T(8,128)(2,1)} %bitcast.46), calls=%async_computation | async-start | bytes 786432 | tf_op jit(solution)/shard_map/all_to_all | solution.py:255
  21.4 11.6 %collective-permute-start.2 = (bf16[768,256]{1,0:T(8,128)(2,1)S(1)}, bf16[768,256]{1,0:T(8,128)(2,1)S(1)}, u32[]{:S(2)}, u32[]{:S(2)}) collective-permute-start(bf16[768,256]{1,0:T(8,128)(2,1)S(1)} %bitcast.53), channel_id=1, source_target_pairs={{0,56},{8,0},{16,8},{24,16},{32,24},{40,32},{48,40},{56,48},{1,57}... | collective-permute-start | bytes 1179656 | tf_op jit(solution)/shard_map/ppermute | solution.py:272
  27.0 9.6 %collective-permute-start = (bf16[768,256]{1,0:T(8,128)(2,1)S(1)}, bf16[768,256]{1,0:T(8,128)(2,1)S(1)}, u32[]{:S(2)}, u32[]{:S(2)}) collective-permute-start(bf16[768,256]{1,0:T(8,128)(2,1)S(1)} %bitcast.54), channel_id=1, source_target_pairs={{0,8},{8,16},{16,24},{24,32},{32,40},{40,48},{48,56},{56,0},{1,9},... | collective-permute-start | bytes 1179656 | tf_op jit(solution)/shard_map/ppermute | solution.py:272
  27.7 8.9 %collective-permute-start.4 = (bf16[192,1024]{1,0:T(8,128)(2,1)S(1)}, bf16[192,1024]{1,0:T(8,128)(2,1)S(1)}, u32[]{:S(2)}, u32[]{:S(2)}) collective-permute-start(bf16[192,1024]{1,0:T(8,128)(2,1)S(1)} %bitcast.47), channel_id=1, source_target_pairs={{0,4},{4,0},{1,5},{5,1},{2,6},{6,2},{3,7},{7,3},{8,12},{12,8},{9,1... | collective-permute-start | bytes 1179656 | tf_op jit(solution)/shard_map/ppermute | solution.py:256
  33.0 12.3 %collective-permute-start.3 = (bf16[768,256]{1,0:T(8,128)(2,1)S(1)}, bf16[768,256]{1,0:T(8,128)(2,1)S(1)}, u32[]{:S(2)}, u32[]{:S(2)}) collective-permute-start(bf16[768,256]{1,0:T(8,128)(2,1)S(1)} %collective-permute-done.2.refs_9_), channel_id=1, source_target_pairs={{0,56},{8,0},{16,8},{24,16},{32,24},{40,32},{48,40},{56,48},{1,57}... | collective-permute-start | bytes 1179656 | tf_op jit(solution)/shard_map/ppermute | solution.py:276
  36.6 8.7 %collective-permute-start.1 = (bf16[768,256]{1,0:T(8,128)(2,1)S(1)}, bf16[768,256]{1,0:T(8,128)(2,1)S(1)}, u32[]{:S(2)}, u32[]{:S(2)}) collective-permute-start(bf16[768,256]{1,0:T(8,128)(2,1)S(1)} %collective-permute-done.refs_8_), channel_id=1, source_target_pairs={{0,8},{8,16},{16,24},{24,32},{32,40},{40,48},{48,56},{56,0},{1,9},... | collective-permute-start | bytes 1179656 | tf_op jit(solution)/shard_map/ppermute | solution.py:276
  45.3 8.5 %collective-permute-start.5 = (bf16[768,256]{1,0:T(8,128)(2,1)S(1)}, bf16[768,256]{1,0:T(8,128)(2,1)S(1)}, u32[]{:S(2)}, u32[]{:S(2)}) collective-permute-start(bf16[768,256]{1,0:T(8,128)(2,1)S(1)} %collective-permute-done.1.refs_7_), channel_id=1, source_target_pairs={{0,8},{8,16},{16,24},{24,32},{32,40},{40,48},{48,56},{56,0},{1,9},... | collective-permute-start | bytes 1179656 | tf_op jit(solution)/shard_map/ppermute | solution.py:276
  45.4 8.4 %collective-permute-start.6 = (bf16[768,256]{1,0:T(8,128)(2,1)S(1)}, bf16[768,256]{1,0:T(8,128)(2,1)S(1)}, u32[]{:S(2)}, u32[]{:S(2)}) collective-permute-start(bf16[768,256]{1,0:T(8,128)(2,1)S(1)} %collective-permute-done.3.refs_8_), channel_id=1, source_target_pairs={{0,56},{8,0},{16,8},{24,16},{32,24},{40,32},{48,40},{56,48},{1,57}... | collective-permute-start | bytes 1179656 | tf_op jit(solution)/shard_map/ppermute | solution.py:276
  53.8 8.1 %collective-permute-start.7 = (bf16[384,256]{1,0:T(8,128)(2,1)S(1)}, bf16[384,256]{1,0:T(8,128)(2,1)S(1)}, u32[]{:S(2)}, u32[]{:S(2)}) collective-permute-start(bf16[384,256]{1,0:T(8,128)(2,1)S(1)} %slice.66), channel_id=1, source_target_pairs={{0,8},{8,16},{16,24},{24,32},{32,40},{40,48},{48,56},{56,0},{1,9},... | collective-permute-start | bytes 589832 | tf_op jit(solution)/shard_map/ppermute | solution.py:279
  53.9 8.0 %collective-permute-start.8 = (bf16[384,256]{1,0:T(8,128)(2,1)S(1)}, bf16[384,256]{1,0:T(8,128)(2,1)S(1)}, u32[]{:S(2)}, u32[]{:S(2)}) collective-permute-start(bf16[384,256]{1,0:T(8,128)(2,1)S(1)} %slice.67), channel_id=1, source_target_pairs={{0,56},{8,0},{16,8},{24,16},{32,24},{40,32},{48,40},{56,48},{1,57}... | collective-permute-start | bytes 589832 | tf_op jit(solution)/shard_map/ppermute | solution.py:279
  64.4 8.5 %collective-permute-start.9 = (f32[2,136,768]{2,1,0:T(8,128)S(1)}, f32[2,136,768]{2,1,0:T(8,128)S(1)}, u32[]{:S(2)}, u32[]{:S(2)}) collective-permute-start(f32[2,136,768]{2,1,0:T(8,128)S(1)} %attend.9), channel_id=1, source_target_pairs={{0,4},{4,0},{1,5},{5,1},{2,6},{6,2},{3,7},{7,3},{8,12},{12,8},{9,1... | collective-permute-start | bytes 2506760 | tf_op jit(solution)/shard_map/ppermute | solution.py:286
where the time goes:
time: 87.2 us; the launch traced here: 86.3 us
  starting transfers between devices  35.5 us (41%)
  Pallas kernels  24.5 us (28%)
  blocking collectives  12.3 us (14%)
  waiting for transfers between devices  6.49 us (7%)
  local copies, waits for them, and re-layouts  5.8 us (7%)
  other arithmetic  1.31 us (2%)
    pallas_call x5, Pallas kernels, attend(): pl.pallas_call(functools.partial(attend_kernel, counts, first, sides), ou...  24.3 us
    all_to_all x1, blocking collectives, attention(): return lax.all_to_all(result, 'tp', split_axis=0, concat_axis=1, tiled=True)  12.3 us
    all_to_all x1, starting transfers between devices, attention(): lax.all_to_all(spread, ('x', 'tp'), split_axis=0, concat_axis=0, tiled=True)  7.7 us
    ppermute x2, starting transfers between devices, attention(): lax.ppermute(down, 'z', shift(NZ, -1))  6.66 us
    ppermute x1, starting transfers between devices, attention(): theirs = lax.ppermute(sent, 'c', shift(2, 1))  5.92 us
    ppermute x1, starting transfers between devices, attention(): lax.ppermute(line, 'z', shift(NZ, -1))  5.65 us
    all_to_all x1, waiting for transfers between devices, attention(): lax.all_to_all(spread, ('x', 'tp'), split_axis=0, concat_axis=0, tiled=True)  4.48 us
    all_to_all x1, starting transfers between devices, attention(): lax.all_to_all(queries, 'tp', split_axis=1, concat_axis=0, tiled=True)  3.46 us
  transfers between devices with their start and end apart: 12, of which 2 were waited for; matrix products, arithmetic and copies ran while one was open for 3% of the time, Pallas kernels for 25%

commit v1 on v0

--- a/solution.py
+++ b/solution.py
@@ -39,15 +39,11 @@
         before = refs[at : at + len(sides)]
         at += len(sides)
     outs = refs[at : at + len(sides)]
-    kv, q_turned, work, sems = refs[at + len(sides) :]
-    copies, row = [], 0
-    for i, n in enumerate(counts):
-        copy = pltpu.make_async_copy(pieces[i], kv.at[pl.ds(row * BLOCK, n * BLOCK)], sems.at[i])
-        copy.start()
-        copies.append(copy)
-        row += n
-    for copy in copies:
-        copy.wait()
+    kv, q_turned, work = refs[at + len(sides) :]
+    row = 0
+    for piece, n in zip(pieces, counts):
+        kv[row : row + n * BLOCK] = piece[...]
+        row += n * BLOCK
 
     def fetch(qb, place, width):
         offs = [pl.multiple_of(idx[qb, place + j] * BLOCK, BLOCK) for j in range(width)]
@@ -181,19 +177,17 @@
     first = state is None
     smem = pl.BlockSpec(memory_space=pltpu.SMEM)
     vmem = pl.BlockSpec(memory_space=pltpu.VMEM)
-    anywhere = pl.BlockSpec(memory_space=pl.ANY)
     held = [] if first else [state[i] for i in sides]
     shape = jax.ShapeDtypeStruct((2, ROWS, LANES), jnp.float32)
     return pl.pallas_call(
         functools.partial(attend_kernel, counts, first, sides),
         out_shape=(shape,) * len(sides),
-        in_specs=[smem] * 5 + [vmem] * len(sides) + [anywhere] * len(pieces) + [vmem] * len(held),
+        in_specs=[smem] * 5 + [vmem] * len(sides) + [vmem] * len(pieces) + [vmem] * len(held),
         out_specs=(vmem,) * len(sides),
         scratch_shapes=[
             pltpu.VMEM((total * BLOCK, 2 * HEAD), jnp.bfloat16),
             pltpu.VMEM((HEAD, LANES), jnp.bfloat16),
             pltpu.VMEM((ROWS, LANES), jnp.float32),
-            pltpu.SemaphoreType.DMA((len(pieces),)),
         ],
         compiler_params=pltpu.CompilerParams(vmem_limit_bytes=32 * 1024 * 1024),
         cost_estimate=pl.CostEstimate(
@@ -218,7 +212,8 @@
     return cnt, jnp.cumsum(cnt, 0) - cnt, idx, kpos
 
 
-def merge_kernel(mine, theirs, out):
+def merge_kernel(me, mine, theirs, *refs):
+    outs, rows_ref = refs[:4], refs[4]
     for b in range(2):
         m1, m2 = mine[b, HEAD : HEAD + 1], theirs[b, HEAD : HEAD + 1]
         top = jnp.maximum(m1, m2)
@@ -228,16 +223,60 @@
         o = (mine[b, 0:HEAD] * w1 + theirs[b, 0:HEAD] * w2) / denom
         rows = o.T.astype(jnp.bfloat16)
         for h in range(GROUP):
-            out[b * BLOCK : (b + 1) * BLOCK, h * HEAD : (h + 1) * HEAD] = rows[h * BLOCK : (h + 1) * BLOCK]
-
-
-def merge(mine, theirs):
+            rows_ref[b * BLOCK : (b + 1) * BLOCK, h * HEAD : (h + 1) * HEAD] = rows[h * BLOCK : (h + 1) * BLOCK]
+    count = outs[0].shape[0]
+    for k, out in enumerate(outs):
+        out[...] = rows_ref[pl.ds(pl.multiple_of(lax.rem(me[0] + k, 4) * count, count), count)]
+
+
+def merge(me, mine, theirs, rows):
+    vmem = pl.BlockSpec(memory_space=pltpu.VMEM)
     return pl.pallas_call(
         merge_kernel,
-        out_shape=jax.ShapeDtypeStruct((2 * BLOCK, GROUP * HEAD), jnp.bfloat16),
+        out_shape=(jax.ShapeDtypeStruct((rows, GROUP * HEAD), jnp.bfloat16),) * 4,
+        in_specs=[pl.BlockSpec(memory_space=pltpu.SMEM), vmem, vmem],
+        out_specs=(vmem,) * 4,
+        scratch_shapes=[pltpu.VMEM((2 * BLOCK, GROUP * HEAD), jnp.bfloat16)],
         compiler_params=pltpu.CompilerParams(vmem_limit_bytes=16 * 1024 * 1024),
         name="merge",
-    )(mine, theirs)
+    )(me, mine, theirs)
+
+
+def join_kernel(me, *refs):
+    out = refs[4]
+    width = GROUP * HEAD
+    for k in range(4):
+        out[:, pl.ds(pl.multiple_of(lax.rem(me[0] + 4 - k, 4) * width, width), width)] = refs[k][...]
+
+
+def join(me, parts):
+    vmem = pl.BlockSpec(memory_space=pltpu.VMEM)
+    return pl.pallas_call(
+        join_kernel,
+        out_shape=jax.ShapeDtypeStruct((parts[0].shape[0], 4 * GROUP * HEAD), jnp.bfloat16),
+        in_specs=[pl.BlockSpec(memory_space=pltpu.SMEM)] + [vmem] * 4,
+        out_specs=vmem,
+        compiler_params=pltpu.CompilerParams(vmem_limit_bytes=8 * 1024 * 1024),
+        name="join",
+    )(me, *parts)
+
+
+def spread_kernel(keys, values, out):
+    for h in range(KEY_VALUE_HEADS):
+        sl = slice(h * HEAD, (h + 1) * HEAD)
+        k, v = keys[:, sl], values[:, sl]
+        for i in range(NX):
+            out[i * KEY_VALUE_HEADS + h, :, 0:HEAD] = k
+            out[i * KEY_VALUE_HEADS + h, :, HEAD : 2 * HEAD] = v
+
+
+def spread(keys, values):
+    return pl.pallas_call(
+        spread_kernel,
+        out_shape=jax.ShapeDtypeStruct((NX * KEY_VALUE_HEADS, keys.shape[0], 2 * HEAD), jnp.bfloat16),
+        compiler_params=pltpu.CompilerParams(vmem_limit_bytes=4 * 1024 * 1024),
+        name="spread",
+    )(keys, values)
 
 
 def lookup(block_order, index):
@@ -248,9 +287,8 @@
 def attention(queries, keys, values, block_order):
     rows = queries.shape[0]
     x, z, c = lax.axis_index("x"), lax.axis_index("z"), lax.axis_index("c")
-    pair = jnp.concatenate([keys.reshape(rows, 4, HEAD), values.reshape(rows, 4, HEAD)], 2).transpose(1, 0, 2)
-    spread = jnp.broadcast_to(pair[None], (NX, 4, rows, 2 * HEAD)).reshape(NX * 4, rows, 2 * HEAD)
-    line = lax.all_to_all(spread, ("x", "tp"), split_axis=0, concat_axis=0, tiled=True).reshape(-1, 2 * HEAD)
+    line = lax.all_to_all(spread(keys, values), ("x", "tp"), split_axis=0, concat_axis=0, tiled=True)
+    line = line.reshape(-1, 2 * HEAD)
 
     q_own = lax.all_to_all(queries, "tp", split_axis=1, concat_axis=0, tiled=True)
     q_other = lax.ppermute(q_own, "c", shift(2, 1))
@@ -285,8 +323,10 @@
     (sent,) = attend(part, qpos, (q_own, q_other), pieces, state, (1,))
     theirs = lax.ppermute(sent, "c", shift(2, 1))
     (mine,) = attend(part, qpos, (q_own, q_other), pieces, state, (0,))
-    result = merge(mine, theirs)
-    return lax.all_to_all(result, "tp", split_axis=0, concat_axis=1, tiled=True)
+    me = lax.axis_index("tp").reshape(1)
+    parts = merge(me, mine, theirs, rows)
+    parts = [parts[0]] + [lax.ppermute(parts[k], "tp", shift(4, k)) for k in range(1, 4)]
+    return join(me, parts)
 
 
 def solution(mesh):

time: 87.2 us -> 83.3 us (0.955)
  blocking collectives: 12.3 us -> 0 us
  starting transfers between devices: 35.5 us -> 42.1 us
  waiting for transfers between devices: 6.49 us -> 10.3 us
    all_to_all x1 -> x0, blocking collectives: 12.3 us -> none  [attention(): return lax.all_to_all(result, 'tp', split_axis=0, concat_axis=1, tiled=True)]
    ppermute x0 -> x3, starting transfers between devices: none -> 5.38 us  [attention(): lax.ppermute(parts[k], 'tp', shift(4, k))]
    ppermute x0 -> x3, waiting for transfers between devices: none -> 3.52 us  [attention(): lax.ppermute(parts[k], 'tp', shift(4, k))]
    pallas_call x5, Pallas kernels: 24.3 us -> 22.1 us  [attend(): pl.pallas_call(functools.partial(attend_kernel, counts, first, sides), ou...]
    pallas_call x1 -> x3, Pallas kernels: 0.22 us -> 1.85 us  [the longest x1 0.8 us: spread(): pl.pallas_call(spread_kernel, out_shape=jax.ShapeDtypeStruct((NX * KEY_VA...]
    unnamed x20 -> x22, local copies, waits for them, and re-layouts: 2.41 us -> 4.01 us
    ppermute x1, starting transfers between devices: 5.92 us -> 7.15 us  [attention(): theirs = lax.ppermute(sent, 'c', shift(2, 1))]
  transfers between devices with their start and end apart: 12 -> 15, of which waited for: 2 -> 5; matrix products, arithmetic and copies ran while one was open for 3% -> 3% of each run, Pallas kernels for 25% -> 24%
where the time goes in v1:
time: 83.3 us; the launch traced here: 82.9 us
  starting transfers between devices  42.1 us (51%)
  Pallas kernels  24 us (29%)
  waiting for transfers between devices  10.3 us (12%)
  local copies, waits for them, and re-layouts  4.99 us (6%)
  other arithmetic  1.26 us (2%)
    pallas_call x5, Pallas kernels, attend(): pl.pallas_call(functools.partial(attend_kernel, counts, first, sides), ou...  22.1 us
    all_to_all x1, starting transfers between devices, attention(): lax.all_to_all(spread(keys, values), ('x', 'tp'), split_axis=0, concat_ax...  7.7 us
    ppermute x1, starting transfers between devices, attention(): theirs = lax.ppermute(sent, 'c', shift(2, 1))  7.15 us
    ppermute x2, starting transfers between devices, attention(): lax.ppermute(down, 'z', shift(NZ, -1))  6.47 us
    ppermute x1, starting transfers between devices, attention(): lax.ppermute(line, 'z', shift(NZ, -1))  5.65 us
    ppermute x3, starting transfers between devices, attention(): lax.ppermute(parts[k], 'tp', shift(4, k))  5.38 us
    all_to_all x1, waiting for transfers between devices, attention(): lax.all_to_all(spread(keys, values), ('x', 'tp'), split_axis=0, concat_ax...  4.48 us
    unnamed x22, local copies, waits for them, and re-layouts  4.01 us
  transfers between devices with their start and end apart: 15, of which 5 were waited for; matrix products, arithmetic and copies ran while one was open for 3% of the time, Pallas kernels for 24%

profile of v1, /device:TPU:1, one launch (start us, length us, event | category | flops | bytes accessed | tf_op | source)
XLA Modules:
  0.0 82.9 jit_solution(16226904347403569090)
XLA Ops:
  0.0 0.0 copy-start
  0.0 0.8 copy-done
  0.8 0.0 copy-start.1
  0.8 0.8 copy-done.1
  1.6 0.8 spread.1
  2.4 0.0 copy-start.5
  2.4 0.0 copy-start.2
  2.4 7.7 %all-to-all-start.1 = ((bf16[16,48,256]{2,1,0:T(8,128)(2,1)}), bf16[16,48,256]{2,1,0:T(8,128)(2,1)S(1)}, u32[]{:S(2)}, u32[]{:S(2)}) async-start(bf16[16,48,256]{2,1,0:T(8,128)(2,1)} %spread.1), calls=%async_computation.1 | async-start | bytes 786432 | tf_op jit(solution)/shard_map/all_to_all | solution.py:290
  10.1 0.0 copy-start.4
  10.1 0.0 copy-start.3
  10.1 0.0 copy-done.5
  10.2 0.6 copy-done.4
  10.8 0.0 copy-done.3
  10.8 0.1 eq.60
  10.9 0.6 copy-done.9
  11.5 0.0 copy-start.10
  11.5 0.2 select_reduce_fusion.2
  11.7 0.5 copy-done.10
  12.2 0.1 reshape.38
  12.2 0.0 copy-done.2
  12.2 0.8 copy.16
  13.0 0.6 copy-done.6
  13.7 0.0 copy-done.7
  13.7 0.0 copy-done.8
  13.7 0.2 select_reduce_fusion.3.refs_4_
  13.9 4.5 %all-to-all-done.1 = bf16[16,48,256]{2,1,0:T(8,128)(2,1)S(1)} async-done(((bf16[16,48,256]{2,1,0:T(8,128)(2,1)}), bf16[16,48,256]{2,1,0:T(8,128)(2,1)S(1)}, u32[]{:S(2)}, u32[]{:S(2)}) %all-to-all-start.1) | async-done | bytes 393248 | tf_op jit(solution)/shard_map/all_to_all | solution.py:290
  18.4 3.5 %all-to-all-start = ((bf16[48,4,1024]{2,0,1:T(8,128)(2,1)}), bf16[48,4,1024]{2,0,1:T(8,128)(2,1)S(1)}, u32[]{:S(2)}, u32[]{:S(2)}) async-start(bf16[48,4,1024]{2,0,1:T(8,128)(2,1)} %bitcast.40), calls=%async_computation | async-start | bytes 786432 | tf_op jit(solution)/shard_map/all_to_all | solution.py:293
  21.8 0.2 compare_select_fusion
  22.1 5.7 %collective-permute-start.2 = (bf16[768,256]{1,0:T(8,128)(2,1)S(1)}, bf16[768,256]{1,0:T(8,128)(2,1)S(1)}, u32[]{:S(2)}, u32[]{:S(2)}) collective-permute-start(bf16[768,256]{1,0:T(8,128)(2,1)S(1)} %bitcast.46), channel_id=1, source_target_pairs={{0,56},{8,0},{16,8},{24,16},{32,24},{40,32},{48,40},{56,48},{1,57}... | collective-permute-start | bytes 1179656 | tf_op jit(solution)/shard_map/ppermute | solution.py:310
  27.7 0.0 collective-permute-start
  27.7 0.5 convert_reduce_fusion
  28.2 0.2 select_reduce_fusion
  28.4 0.0 all-to-all-done
  28.4 3.3 %collective-permute-start.4 = (bf16[192,1024]{1,0:T(8,128)(2,1)S(1)}, bf16[192,1024]{1,0:T(8,128)(2,1)S(1)}, u32[]{:S(2)}, u32[]{:S(2)}) collective-permute-start(bf16[192,1024]{1,0:T(8,128)(2,1)S(1)} %bitcast.41), channel_id=1, source_target_pairs={{0,4},{4,0},{1,5},{5,1},{2,6},{6,2},{3,7},{7,3},{8,12},{12,8},{9,1... | collective-permute-start | bytes 1179656 | tf_op jit(solution)/shard_map/ppermute | solution.py:294
  31.7 2.0 %collective-permute-done.2.refs_9_ = bf16[768,256]{1,0:T(8,128)(2,1)S(1)} collective-permute-done((bf16[768,256]{1,0:T(8,128)(2,1)S(1)}, bf16[768,256]{1,0:T(8,128)(2,1)S(1)}, u32[]{:S(2)}, u32[]{:S(2)}) %collective-permute-start.2) | collective-permute-done | bytes 393248 | tf_op jit(solution)/shard_map/ppermute | solution.py:310
  33.7 3.6 %collective-permute-start.3 = (bf16[768,256]{1,0:T(8,128)(2,1)S(1)}, bf16[768,256]{1,0:T(8,128)(2,1)S(1)}, u32[]{:S(2)}, u32[]{:S(2)}) collective-permute-start(bf16[768,256]{1,0:T(8,128)(2,1)S(1)} %collective-permute-done.2.refs_9_), channel_id=1, source_target_pairs={{0,56},{8,0},{16,8},{24,16},{32,24},{40,32},{48,40},{56,48},{1,57}... | collective-permute-start | bytes 1179656 | tf_op jit(solution)/shard_map/ppermute | solution.py:314
  37.3 0.0 collective-permute-done.refs_8_
  37.3 0.0 collective-permute-start.1
  37.3 0.0 collective-permute-done.4.refs_6_.refs_5_
  37.3 8.1 %attend.5 = (f32[2,136,768]{2,1,0:T(8,128)S(1)}, f32[2,136,768]{2,1,0:T(8,128)S(1)}) custom-call(s32[4]{0:T(128)S(1)} %get-tuple-element.74.refs_0_, s32[4]{0:T(128)S(1)} %get-tuple-element.63.refs_1_, s32[4,24]{1,0:T(4,128)S(1)} %get-tuple-element.70.refs_2_, s32[4,24]{1,0:T(4,128)S(1)} %get-tuple-element.53.refs_3_, s32[4]{0:T(128)S(1)} %select_reduce_fusion.3.refs_4_, ...), custom_call_target="tpu_custom_call" | custom-call | flops 1811939328 | bytes 2850816 | tf_op jit(solution)/shard_map/attend/pallas_call | solution.py:182
  45.4 0.0 collective-permute-done.3.refs_8_
  45.4 0.3 collective-permute-done.1.refs_7_
  45.7 0.0 collective-permute-start.5
  45.7 2.9 %collective-permute-start.6 = (bf16[768,256]{1,0:T(8,128)(2,1)S(1)}, bf16[768,256]{1,0:T(8,128)(2,1)S(1)}, u32[]{:S(2)}, u32[]{:S(2)}) collective-permute-start(bf16[768,256]{1,0:T(8,128)(2,1)S(1)} %collective-permute-done.3.refs_8_), channel_id=1, source_target_pairs={{0,56},{8,0},{16,8},{24,16},{32,24},{40,32},{48,40},{56,48},{1,57}... | collective-permute-start | bytes 1179656 | tf_op jit(solution)/shard_map/ppermute | solution.py:314
  48.6 5.0 %attend.6 = (f32[2,136,768]{2,1,0:T(8,128)S(1)}, f32[2,136,768]{2,1,0:T(8,128)S(1)}) custom-call(s32[4]{0:T(128)S(1)} %get-tuple-element.75.refs_0_, s32[4]{0:T(128)S(1)} %get-tuple-element.62.refs_1_, s32[4,24]{1,0:T(4,128)S(1)} %get-tuple-element.71.refs_2_, s32[4,24]{1,0:T(4,128)S(1)} %get-tuple-element.52.refs_3_, s32[4]{0:T(128)S(1)} %select_reduce_fusion.3.refs_4_, ...), custom_call_target="tpu_custom_call" | custom-call | flops 1207959552 | bytes 2457600 | tf_op jit(solution)/shard_map/attend/pallas_call | solution.py:182
  53.6 0.0 collective-permute-done.5.refs_7_
  53.6 0.0 collective-permute-done.6.refs_8_
  53.6 0.1 collective-permute-start.7
  53.7 2.9 %collective-permute-start.8 = (bf16[384,256]{1,0:T(8,128)(2,1)S(1)}, bf16[384,256]{1,0:T(8,128)(2,1)S(1)}, u32[]{:S(2)}, u32[]{:S(2)}) collective-permute-start(bf16[384,256]{1,0:T(8,128)(2,1)S(1)} %slice.67), channel_id=1, source_target_pairs={{0,56},{8,0},{16,8},{24,16},{32,24},{40,32},{48,40},{56,48},{1,57}... | collective-permute-start | bytes 589832 | tf_op jit(solution)/shard_map/ppermute | solution.py:317
  56.6 5.0 %attend.7 = (f32[2,136,768]{2,1,0:T(8,128)S(1)}, f32[2,136,768]{2,1,0:T(8,128)S(1)}) custom-call(s32[4]{0:T(128)S(1)} %get-tuple-element.76.refs_0_, s32[4]{0:T(128)S(1)} %get-tuple-element.61.refs_1_, s32[4,24]{1,0:T(4,128)S(1)} %get-tuple-element.72.refs_2_, s32[4,24]{1,0:T(4,128)S(1)} %get-tuple-element.51.refs_3_, s32[4]{0:T(128)S(1)} %select_reduce_fusion.3.refs_4_, ...), custom_call_target="tpu_custom_call" | custom-call | flops 1207959552 | bytes 2457600 | tf_op jit(solution)/shard_map/attend/pallas_call | solution.py:182
  61.6 0.0 collective-permute-done.7.refs_6_
  61.6 0.0 collective-permute-done.8.refs_7_
  61.6 2.0 %attend.9 = f32[2,136,768]{2,1,0:T(8,128)S(1)} custom-call(s32[4]{0:T(128)S(1)} %get-tuple-element.73.refs_0_, s32[4]{0:T(128)S(1)} %get-tuple-element.64.refs_1_, s32[4,24]{1,0:T(4,128)S(1)} %get-tuple-element.69.refs_2_, s32[4,24]{1,0:T(4,128)S(1)} %get-tuple-element.54.refs_3_, s32[4]{0:T(128)S(1)} %select_reduce_fusion.3.refs_4_, ...), custom_call_target="tpu_custom_call" | custom-call | flops 301989888 | bytes 2064384 | tf_op jit(solution)/shard_map/attend/pallas_call | solution.py:182
  63.7 7.2 %collective-permute-start.9 = (f32[2,136,768]{2,1,0:T(8,128)S(1)}, f32[2,136,768]{2,1,0:T(8,128)S(1)}, u32[]{:S(2)}, u32[]{:S(2)}) collective-permute-start(f32[2,136,768]{2,1,0:T(8,128)S(1)} %attend.9), channel_id=1, source_target_pairs={{0,4},{4,0},{1,5},{5,1},{2,6},{6,2},{3,7},{7,3},{8,12},{12,8},{9,1... | collective-permute-start | bytes 2506760 | tf_op jit(solution)/shard_map/ppermute | solution.py:324
  70.8 2.0 %attend.8.mine = f32[2,136,768]{2,1,0:T(8,128)S(1)} custom-call(s32[4]{0:T(128)S(1)} %get-tuple-element.73.refs_0_, s32[4]{0:T(128)S(1)} %get-tuple-element.64.refs_1_, s32[4,24]{1,0:T(4,128)S(1)} %get-tuple-element.69.refs_2_, s32[4,24]{1,0:T(4,128)S(1)} %get-tuple-element.54.refs_3_, s32[4]{0:T(128)S(1)} %select_reduce_fusion.3.refs_4_, ...), custom_call_target="tpu_custom_call" | custom-call | flops 301989888 | bytes 2064384 | tf_op jit(solution)/shard_map/attend/pallas_call | solution.py:182
  72.9 0.0 collective-permute-done.9.theirs
  72.9 0.3 merge.1
  73.2 1.8 %collective-permute-start.10 = (bf16[48,1024]{1,0:T(8,128)(2,1)S(1)}, bf16[48,1024]{1,0:T(8,128)(2,1)S(1)}, u32[]{:S(2)}, u32[]{:S(2)}) collective-permute-start(bf16[48,1024]{1,0:T(8,128)(2,1)S(1)} %get-tuple-element.46), channel_id=1, source_target_pairs={{0,1},{1,2},{2,3},{3,0},{4,5},{5,6},{6,7},{7,4},{8,9},{9,10},{10,1... | collective-permute-start | bytes 294920 | tf_op jit(solution)/shard_map/ppermute | solution.py:328
  75.0 2.4 %collective-permute-start.11 = (bf16[48,1024]{1,0:T(8,128)(2,1)S(1)}, bf16[48,1024]{1,0:T(8,128)(2,1)S(1)}, u32[]{:S(2)}, u32[]{:S(2)}) collective-permute-start(bf16[48,1024]{1,0:T(8,128)(2,1)S(1)} %get-tuple-element.47), channel_id=1, source_target_pairs={{0,2},{1,3},{2,0},{3,1},{4,6},{5,7},{6,4},{7,5},{8,10},{9,11},{10,... | collective-permute-start | bytes 294920 | tf_op jit(solution)/shard_map/ppermute | solution.py:328
  77.4 1.2 %collective-permute-start.12 = (bf16[48,1024]{1,0:T(8,128)(2,1)S(1)}, bf16[48,1024]{1,0:T(8,128)(2,1)S(1)}, u32[]{:S(2)}, u32[]{:S(2)}) collective-permute-start(bf16[48,1024]{1,0:T(8,128)(2,1)S(1)} %get-tuple-element.48), channel_id=1, source_target_pairs={{0,3},{1,0},{2,1},{3,2},{4,7},{5,4},{6,5},{7,6},{8,11},{9,8},{10,9... | collective-permute-start | bytes 294920 | tf_op jit(solution)/shard_map/ppermute | solution.py:328
  78.6 0.5 collective-permute-done.10.refs_1_
  79.0 3.0 %collective-permute-done.11.refs_2_ = bf16[48,1024]{1,0:T(8,128)(2,1)S(1)} collective-permute-done((bf16[48,1024]{1,0:T(8,128)(2,1)S(1)}, bf16[48,1024]{1,0:T(8,128)(2,1)S(1)}, u32[]{:S(2)}, u32[]{:S(2)}) %collective-permute-start.11) | collective-permute-done | bytes 98336 | tf_op jit(solution)/shard_map/ppermute | solution.py:328
  82.1 0.0 collective-permute-done.12.refs_3_
  82.1 0.8 join.1
  (14 shorter events, 0.1 us)
Async XLA Ops:
  0.0 0.8 copy-start
  0.8 0.8 copy-start.1
  2.4 7.8 %copy-start.5 = (s32[4,24]{1,0:T(4,128)S(1)}, s32[4,24]{1,0:T(4,128)}, u32[]{:S(2)}) copy-start(s32[4,24]{1,0:T(4,128)} %constant.65.clone) | copy-start | bytes 1156
  2.4 9.8 %copy-start.2 = (bf16[48,4096]{1,0:T(8,128)(2,1)S(1)}, bf16[48,4096]{1,0:T(8,128)(2,1)}, u32[]{:S(2)}) copy-start(bf16[48,4096]{1,0:T(8,128)(2,1)} %param.11) | copy-start | bytes 1179652
  2.4 16.0 %all-to-all-start.1 = ((bf16[16,48,256]{2,1,0:T(8,128)(2,1)}), bf16[16,48,256]{2,1,0:T(8,128)(2,1)S(1)}, u32[]{:S(2)}, u32[]{:S(2)}) async-start(bf16[16,48,256]{2,1,0:T(8,128)(2,1)} %spread.1), calls=%async_computation.1 | async-start | bytes 786432 | tf_op jit(solution)/shard_map/all_to_all | solution.py:290
  10.1 0.7 copy-start.4
  10.1 0.7 copy-start.3
  10.8 0.7 copy-start.9
  11.5 0.7 copy-start.10
  13.0 0.7 copy-start.6
  13.0 0.7 copy-start.7
  13.0 0.7 copy-start.8
  18.4 10.0 %all-to-all-start = ((bf16[48,4,1024]{2,0,1:T(8,128)(2,1)}), bf16[48,4,1024]{2,0,1:T(8,128)(2,1)S(1)}, u32[]{:S(2)}, u32[]{:S(2)}) async-start(bf16[48,4,1024]{2,0,1:T(8,128)(2,1)} %bitcast.40), calls=%async_computation | async-start | bytes 786432 | tf_op jit(solution)/shard_map/all_to_all | solution.py:293
  22.1 11.6 %collective-permute-start.2 = (bf16[768,256]{1,0:T(8,128)(2,1)S(1)}, bf16[768,256]{1,0:T(8,128)(2,1)S(1)}, u32[]{:S(2)}, u32[]{:S(2)}) collective-permute-start(bf16[768,256]{1,0:T(8,128)(2,1)S(1)} %bitcast.46), channel_id=1, source_target_pairs={{0,56},{8,0},{16,8},{24,16},{32,24},{40,32},{48,40},{56,48},{1,57}... | collective-permute-start | bytes 1179656 | tf_op jit(solution)/shard_map/ppermute | solution.py:310
  27.7 9.6 %collective-permute-start = (bf16[768,256]{1,0:T(8,128)(2,1)S(1)}, bf16[768,256]{1,0:T(8,128)(2,1)S(1)}, u32[]{:S(2)}, u32[]{:S(2)}) collective-permute-start(bf16[768,256]{1,0:T(8,128)(2,1)S(1)} %bitcast.47), channel_id=1, source_target_pairs={{0,8},{8,16},{16,24},{24,32},{32,40},{40,48},{48,56},{56,0},{1,9},... | collective-permute-start | bytes 1179656 | tf_op jit(solution)/shard_map/ppermute | solution.py:310
  28.4 8.9 %collective-permute-start.4 = (bf16[192,1024]{1,0:T(8,128)(2,1)S(1)}, bf16[192,1024]{1,0:T(8,128)(2,1)S(1)}, u32[]{:S(2)}, u32[]{:S(2)}) collective-permute-start(bf16[192,1024]{1,0:T(8,128)(2,1)S(1)} %bitcast.41), channel_id=1, source_target_pairs={{0,4},{4,0},{1,5},{5,1},{2,6},{6,2},{3,7},{7,3},{8,12},{12,8},{9,1... | collective-permute-start | bytes 1179656 | tf_op jit(solution)/shard_map/ppermute | solution.py:294
  33.7 11.8 %collective-permute-start.3 = (bf16[768,256]{1,0:T(8,128)(2,1)S(1)}, bf16[768,256]{1,0:T(8,128)(2,1)S(1)}, u32[]{:S(2)}, u32[]{:S(2)}) collective-permute-start(bf16[768,256]{1,0:T(8,128)(2,1)S(1)} %collective-permute-done.2.refs_9_), channel_id=1, source_target_pairs={{0,56},{8,0},{16,8},{24,16},{32,24},{40,32},{48,40},{56,48},{1,57}... | collective-permute-start | bytes 1179656 | tf_op jit(solution)/shard_map/ppermute | solution.py:314
  37.3 8.4 %collective-permute-start.1 = (bf16[768,256]{1,0:T(8,128)(2,1)S(1)}, bf16[768,256]{1,0:T(8,128)(2,1)S(1)}, u32[]{:S(2)}, u32[]{:S(2)}) collective-permute-start(bf16[768,256]{1,0:T(8,128)(2,1)S(1)} %collective-permute-done.refs_8_), channel_id=1, source_target_pairs={{0,8},{8,16},{16,24},{24,32},{32,40},{40,48},{48,56},{56,0},{1,9},... | collective-permute-start | bytes 1179656 | tf_op jit(solution)/shard_map/ppermute | solution.py:314
  45.7 7.8 %collective-permute-start.5 = (bf16[768,256]{1,0:T(8,128)(2,1)S(1)}, bf16[768,256]{1,0:T(8,128)(2,1)S(1)}, u32[]{:S(2)}, u32[]{:S(2)}) collective-permute-start(bf16[768,256]{1,0:T(8,128)(2,1)S(1)} %collective-permute-done.1.refs_7_), channel_id=1, source_target_pairs={{0,8},{8,16},{16,24},{24,32},{32,40},{40,48},{48,56},{56,0},{1,9},... | collective-permute-start | bytes 1179656 | tf_op jit(solution)/shard_map/ppermute | solution.py:314
  45.7 7.9 %collective-permute-start.6 = (bf16[768,256]{1,0:T(8,128)(2,1)S(1)}, bf16[768,256]{1,0:T(8,128)(2,1)S(1)}, u32[]{:S(2)}, u32[]{:S(2)}) collective-permute-start(bf16[768,256]{1,0:T(8,128)(2,1)S(1)} %collective-permute-done.3.refs_8_), channel_id=1, source_target_pairs={{0,56},{8,0},{16,8},{24,16},{32,24},{40,32},{48,40},{56,48},{1,57}... | collective-permute-start | bytes 1179656 | tf_op jit(solution)/shard_map/ppermute | solution.py:314
  53.6 8.0 %collective-permute-start.7 = (bf16[384,256]{1,0:T(8,128)(2,1)S(1)}, bf16[384,256]{1,0:T(8,128)(2,1)S(1)}, u32[]{:S(2)}, u32[]{:S(2)}) collective-permute-start(bf16[384,256]{1,0:T(8,128)(2,1)S(1)} %slice.66), channel_id=1, source_target_pairs={{0,8},{8,16},{16,24},{24,32},{32,40},{40,48},{48,56},{56,0},{1,9},... | collective-permute-start | bytes 589832 | tf_op jit(solution)/shard_map/ppermute | solution.py:317
  53.7 7.9 %collective-permute-start.8 = (bf16[384,256]{1,0:T(8,128)(2,1)S(1)}, bf16[384,256]{1,0:T(8,128)(2,1)S(1)}, u32[]{:S(2)}, u32[]{:S(2)}) collective-permute-start(bf16[384,256]{1,0:T(8,128)(2,1)S(1)} %slice.67), channel_id=1, source_target_pairs={{0,56},{8,0},{16,8},{24,16},{32,24},{40,32},{48,40},{56,48},{1,57}... | collective-permute-start | bytes 589832 | tf_op jit(solution)/shard_map/ppermute | solution.py:317
  63.7 9.2 %collective-permute-start.9 = (f32[2,136,768]{2,1,0:T(8,128)S(1)}, f32[2,136,768]{2,1,0:T(8,128)S(1)}, u32[]{:S(2)}, u32[]{:S(2)}) collective-permute-start(f32[2,136,768]{2,1,0:T(8,128)S(1)} %attend.9), channel_id=1, source_target_pairs={{0,4},{4,0},{1,5},{5,1},{2,6},{6,2},{3,7},{7,3},{8,12},{12,8},{9,1... | collective-permute-start | bytes 2506760 | tf_op jit(solution)/shard_map/ppermute | solution.py:324
  73.2 5.9 %collective-permute-start.10 = (bf16[48,1024]{1,0:T(8,128)(2,1)S(1)}, bf16[48,1024]{1,0:T(8,128)(2,1)S(1)}, u32[]{:S(2)}, u32[]{:S(2)}) collective-permute-start(bf16[48,1024]{1,0:T(8,128)(2,1)S(1)} %get-tuple-element.46), channel_id=1, source_target_pairs={{0,1},{1,2},{2,3},{3,0},{4,5},{5,6},{6,7},{7,4},{8,9},{9,10},{10,1... | collective-permute-start | bytes 294920 | tf_op jit(solution)/shard_map/ppermute | solution.py:328
  75.0 7.1 %collective-permute-start.11 = (bf16[48,1024]{1,0:T(8,128)(2,1)S(1)}, bf16[48,1024]{1,0:T(8,128)(2,1)S(1)}, u32[]{:S(2)}, u32[]{:S(2)}) collective-permute-start(bf16[48,1024]{1,0:T(8,128)(2,1)S(1)} %get-tuple-element.47), channel_id=1, source_target_pairs={{0,2},{1,3},{2,0},{3,1},{4,6},{5,7},{6,4},{7,5},{8,10},{9,11},{10,... | collective-permute-start | bytes 294920 | tf_op jit(solution)/shard_map/ppermute | solution.py:328
  77.4 4.7 %collective-permute-start.12 = (bf16[48,1024]{1,0:T(8,128)(2,1)S(1)}, bf16[48,1024]{1,0:T(8,128)(2,1)S(1)}, u32[]{:S(2)}, u32[]{:S(2)}) collective-permute-start(bf16[48,1024]{1,0:T(8,128)(2,1)S(1)} %get-tuple-element.48), channel_id=1, source_target_pairs={{0,3},{1,0},{2,1},{3,2},{4,7},{5,4},{6,5},{7,6},{8,11},{9,8},{10,9... | collective-permute-start | bytes 294920 | tf_op jit(solution)/shard_map/ppermute | solution.py:328

commit v2 on v1

--- a/solution.py
+++ b/solution.py
@@ -261,10 +261,18 @@
     )(me, *parts)
 
 
-def spread_kernel(keys, values, out):
+def spread_kernel(keys, values, out, near_keys, near_values, sems):
+    copies = [
+        pltpu.make_async_copy(keys, near_keys, sems.at[0]),
+        pltpu.make_async_copy(values, near_values, sems.at[1]),
+    ]
+    for copy in copies:
+        copy.start()
+    for copy in copies:
+        copy.wait()
     for h in range(KEY_VALUE_HEADS):
         sl = slice(h * HEAD, (h + 1) * HEAD)
-        k, v = keys[:, sl], values[:, sl]
+        k, v = near_keys[:, sl], near_values[:, sl]
         for i in range(NX):
             out[i * KEY_VALUE_HEADS + h, :, 0:HEAD] = k
             out[i * KEY_VALUE_HEADS + h, :, HEAD : 2 * HEAD] = v
@@ -274,7 +282,14 @@
     return pl.pallas_call(
         spread_kernel,
         out_shape=jax.ShapeDtypeStruct((NX * KEY_VALUE_HEADS, keys.shape[0], 2 * HEAD), jnp.bfloat16),
-        compiler_params=pltpu.CompilerParams(vmem_limit_bytes=4 * 1024 * 1024),
+        in_specs=[pl.BlockSpec(memory_space=pltpu.HBM)] * 2,
+        out_specs=pl.BlockSpec(memory_space=pltpu.VMEM),
+        scratch_shapes=[
+            pltpu.VMEM(keys.shape, keys.dtype),
+            pltpu.VMEM(values.shape, values.dtype),
+            pltpu.SemaphoreType.DMA((2,)),
+        ],
+        compiler_params=pltpu.CompilerParams(vmem_limit_bytes=62 * 1024 * 1024),
         name="spread",
     )(keys, values)
 

time: 83.3 us -> 82.5 us (level)
  local copies, waits for them, and re-layouts: 4.99 us -> 3.4 us
    unnamed x22 -> x18, local copies, waits for them, and re-layouts: 4.01 us -> 2.42 us
    pallas_call x1, Pallas kernels: 0.8 us -> 1.63 us  [spread(): pl.pallas_call(spread_kernel, out_shape=jax.ShapeDtypeStruct((NX * KEY_VA...]
where the time goes in v2:
time: 82.5 us; the launch traced here: 82.1 us
  starting transfers between devices  42.1 us (51%)
  Pallas kernels  24.8 us (30%)
  waiting for transfers between devices  10.3 us (12%)
  local copies, waits for them, and re-layouts  3.4 us (4%)
  other arithmetic  1.26 us (2%)
    pallas_call x5, Pallas kernels, attend(): pl.pallas_call(functools.partial(attend_kernel, counts, first, sides), ou...  22.1 us
    all_to_all x1, starting transfers between devices, attention(): lax.all_to_all(spread(keys, values), ('x', 'tp'), split_axis=0, concat_ax...  7.72 us
    ppermute x1, starting transfers between devices, attention(): theirs = lax.ppermute(sent, 'c', shift(2, 1))  7.15 us
    ppermute x2, starting transfers between devices, attention(): lax.ppermute(down, 'z', shift(NZ, -1))  6.47 us
    ppermute x1, starting transfers between devices, attention(): lax.ppermute(line, 'z', shift(NZ, -1))  5.65 us
    ppermute x3, starting transfers between devices, attention(): lax.ppermute(parts[k], 'tp', shift(4, k))  5.38 us
    all_to_all x1, waiting for transfers between devices, attention(): lax.all_to_all(spread(keys, values), ('x', 'tp'), split_axis=0, concat_ax...  4.48 us
    ppermute x3, waiting for transfers between devices, attention(): lax.ppermute(parts[k], 'tp', shift(4, k))  3.52 us
  transfers between devices with their start and end apart: 15, of which 5 were waited for; matrix products, arithmetic and copies ran while one was open for 3% of the time, Pallas kernels for 24%

profile of v2, /device:TPU:1, one launch (start us, length us, event | category | flops | bytes accessed | tf_op | source)
XLA Modules:
  0.0 82.1 jit_solution(12730520796197145821)
XLA Ops:
  0.0 1.6 %spread.1 = bf16[16,48,256]{2,1,0:T(8,128)(2,1)} custom-call(bf16[48,512]{1,0:T(8,128)(2,1)} %keys.1, bf16[48,512]{1,0:T(8,128)(2,1)} %values.1), custom_call_target="tpu_custom_call" | custom-call | tf_op jit(solution)/shard_map/spread/pallas_call | solution.py:282
  1.6 0.0 copy-start.3
  1.7 0.0 copy-start
  1.7 7.7 %all-to-all-start.1 = ((bf16[16,48,256]{2,1,0:T(8,128)(2,1)}), bf16[16,48,256]{2,1,0:T(8,128)(2,1)S(1)}, u32[]{:S(2)}, u32[]{:S(2)}) async-start(bf16[16,48,256]{2,1,0:T(8,128)(2,1)} %spread.1), calls=%async_computation.1 | async-start | bytes 786432 | tf_op jit(solution)/shard_map/all_to_all | solution.py:305
  9.4 0.0 copy-start.2
  9.4 0.0 copy-start.1
  9.4 0.0 copy-done.3
  9.4 0.6 copy-done.2
  10.1 0.0 copy-done.1
  10.1 0.0 copy-start.7
  10.1 0.1 eq.60
  10.2 0.6 copy-done.7
  10.8 0.0 copy-start.8
  10.8 0.2 select_reduce_fusion.2
  10.9 0.5 copy-done.8
  11.4 0.1 reshape.38
  11.5 0.0 copy-done
  11.5 0.8 copy.16
  12.3 0.0 copy-start.4
  12.3 0.0 copy-start.5
  12.3 0.0 copy-start.6
  12.3 0.6 copy-done.4
  12.9 0.0 copy-done.5
  13.0 0.0 copy-done.6
  13.0 0.2 select_reduce_fusion.3.refs_4_
  13.2 4.5 %all-to-all-done.1 = bf16[16,48,256]{2,1,0:T(8,128)(2,1)S(1)} async-done(((bf16[16,48,256]{2,1,0:T(8,128)(2,1)}), bf16[16,48,256]{2,1,0:T(8,128)(2,1)S(1)}, u32[]{:S(2)}, u32[]{:S(2)}) %all-to-all-start.1) | async-done | bytes 393248 | tf_op jit(solution)/shard_map/all_to_all | solution.py:305
  17.7 3.5 %all-to-all-start = ((bf16[48,4,1024]{2,0,1:T(8,128)(2,1)}), bf16[48,4,1024]{2,0,1:T(8,128)(2,1)S(1)}, u32[]{:S(2)}, u32[]{:S(2)}) async-start(bf16[48,4,1024]{2,0,1:T(8,128)(2,1)} %bitcast.40), calls=%async_computation | async-start | bytes 786432 | tf_op jit(solution)/shard_map/all_to_all | solution.py:308
  21.1 0.2 compare_select_fusion
  21.3 5.7 %collective-permute-start.2 = (bf16[768,256]{1,0:T(8,128)(2,1)S(1)}, bf16[768,256]{1,0:T(8,128)(2,1)S(1)}, u32[]{:S(2)}, u32[]{:S(2)}) collective-permute-start(bf16[768,256]{1,0:T(8,128)(2,1)S(1)} %bitcast.46), channel_id=1, source_target_pairs={{0,56},{8,0},{16,8},{24,16},{32,24},{40,32},{48,40},{56,48},{1,57}... | collective-permute-start | bytes 1179656 | tf_op jit(solution)/shard_map/ppermute | solution.py:325
  27.0 0.0 collective-permute-start
  27.0 0.5 convert_reduce_fusion
  27.5 0.2 select_reduce_fusion
  27.7 0.0 all-to-all-done
  27.7 3.3 %collective-permute-start.4 = (bf16[192,1024]{1,0:T(8,128)(2,1)S(1)}, bf16[192,1024]{1,0:T(8,128)(2,1)S(1)}, u32[]{:S(2)}, u32[]{:S(2)}) collective-permute-start(bf16[192,1024]{1,0:T(8,128)(2,1)S(1)} %bitcast.41), channel_id=1, source_target_pairs={{0,4},{4,0},{1,5},{5,1},{2,6},{6,2},{3,7},{7,3},{8,12},{12,8},{9,1... | collective-permute-start | bytes 1179656 | tf_op jit(solution)/shard_map/ppermute | solution.py:309
  31.0 2.0 %collective-permute-done.2.refs_9_ = bf16[768,256]{1,0:T(8,128)(2,1)S(1)} collective-permute-done((bf16[768,256]{1,0:T(8,128)(2,1)S(1)}, bf16[768,256]{1,0:T(8,128)(2,1)S(1)}, u32[]{:S(2)}, u32[]{:S(2)}) %collective-permute-start.2) | collective-permute-done | bytes 393248 | tf_op jit(solution)/shard_map/ppermute | solution.py:325
  33.0 3.6 %collective-permute-start.3 = (bf16[768,256]{1,0:T(8,128)(2,1)S(1)}, bf16[768,256]{1,0:T(8,128)(2,1)S(1)}, u32[]{:S(2)}, u32[]{:S(2)}) collective-permute-start(bf16[768,256]{1,0:T(8,128)(2,1)S(1)} %collective-permute-done.2.refs_9_), channel_id=1, source_target_pairs={{0,56},{8,0},{16,8},{24,16},{32,24},{40,32},{48,40},{56,48},{1,57}... | collective-permute-start | bytes 1179656 | tf_op jit(solution)/shard_map/ppermute | solution.py:329
  36.6 0.0 collective-permute-done.refs_8_
  36.6 0.0 collective-permute-start.1
  36.6 0.0 collective-permute-done.4.refs_6_.refs_5_
  36.6 8.1 %attend.5 = (f32[2,136,768]{2,1,0:T(8,128)S(1)}, f32[2,136,768]{2,1,0:T(8,128)S(1)}) custom-call(s32[4]{0:T(128)S(1)} %get-tuple-element.74.refs_0_, s32[4]{0:T(128)S(1)} %get-tuple-element.63.refs_1_, s32[4,24]{1,0:T(4,128)S(1)} %get-tuple-element.70.refs_2_, s32[4,24]{1,0:T(4,128)S(1)} %get-tuple-element.53.refs_3_, s32[4]{0:T(128)S(1)} %select_reduce_fusion.3.refs_4_, ...), custom_call_target="tpu_custom_call" | custom-call | flops 1811939328 | bytes 2850816 | tf_op jit(solution)/shard_map/attend/pallas_call | solution.py:182
  44.7 0.0 collective-permute-done.3.refs_8_
  44.7 0.3 collective-permute-done.1.refs_7_
  45.0 0.0 collective-permute-start.5
  45.0 2.9 %collective-permute-start.6 = (bf16[768,256]{1,0:T(8,128)(2,1)S(1)}, bf16[768,256]{1,0:T(8,128)(2,1)S(1)}, u32[]{:S(2)}, u32[]{:S(2)}) collective-permute-start(bf16[768,256]{1,0:T(8,128)(2,1)S(1)} %collective-permute-done.3.refs_8_), channel_id=1, source_target_pairs={{0,56},{8,0},{16,8},{24,16},{32,24},{40,32},{48,40},{56,48},{1,57}... | collective-permute-start | bytes 1179656 | tf_op jit(solution)/shard_map/ppermute | solution.py:329
  47.9 5.0 %attend.6 = (f32[2,136,768]{2,1,0:T(8,128)S(1)}, f32[2,136,768]{2,1,0:T(8,128)S(1)}) custom-call(s32[4]{0:T(128)S(1)} %get-tuple-element.75.refs_0_, s32[4]{0:T(128)S(1)} %get-tuple-element.62.refs_1_, s32[4,24]{1,0:T(4,128)S(1)} %get-tuple-element.71.refs_2_, s32[4,24]{1,0:T(4,128)S(1)} %get-tuple-element.52.refs_3_, s32[4]{0:T(128)S(1)} %select_reduce_fusion.3.refs_4_, ...), custom_call_target="tpu_custom_call" | custom-call | flops 1207959552 | bytes 2457600 | tf_op jit(solution)/shard_map/attend/pallas_call | solution.py:182
  52.8 0.0 collective-permute-done.5.refs_7_
  52.9 0.0 collective-permute-done.6.refs_8_
  52.9 0.1 collective-permute-start.7
  53.0 2.9 %collective-permute-start.8 = (bf16[384,256]{1,0:T(8,128)(2,1)S(1)}, bf16[384,256]{1,0:T(8,128)(2,1)S(1)}, u32[]{:S(2)}, u32[]{:S(2)}) collective-permute-start(bf16[384,256]{1,0:T(8,128)(2,1)S(1)} %slice.67), channel_id=1, source_target_pairs={{0,56},{8,0},{16,8},{24,16},{32,24},{40,32},{48,40},{56,48},{1,57}... | collective-permute-start | bytes 589832 | tf_op jit(solution)/shard_map/ppermute | solution.py:332
  55.9 5.0 %attend.7 = (f32[2,136,768]{2,1,0:T(8,128)S(1)}, f32[2,136,768]{2,1,0:T(8,128)S(1)}) custom-call(s32[4]{0:T(128)S(1)} %get-tuple-element.76.refs_0_, s32[4]{0:T(128)S(1)} %get-tuple-element.61.refs_1_, s32[4,24]{1,0:T(4,128)S(1)} %get-tuple-element.72.refs_2_, s32[4,24]{1,0:T(4,128)S(1)} %get-tuple-element.51.refs_3_, s32[4]{0:T(128)S(1)} %select_reduce_fusion.3.refs_4_, ...), custom_call_target="tpu_custom_call" | custom-call | flops 1207959552 | bytes 2457600 | tf_op jit(solution)/shard_map/attend/pallas_call | solution.py:182
  60.9 0.0 collective-permute-done.7.refs_6_
  60.9 0.0 collective-permute-done.8.refs_7_
  60.9 2.0 %attend.9 = f32[2,136,768]{2,1,0:T(8,128)S(1)} custom-call(s32[4]{0:T(128)S(1)} %get-tuple-element.73.refs_0_, s32[4]{0:T(128)S(1)} %get-tuple-element.64.refs_1_, s32[4,24]{1,0:T(4,128)S(1)} %get-tuple-element.69.refs_2_, s32[4,24]{1,0:T(4,128)S(1)} %get-tuple-element.54.refs_3_, s32[4]{0:T(128)S(1)} %select_reduce_fusion.3.refs_4_, ...), custom_call_target="tpu_custom_call" | custom-call | flops 301989888 | bytes 2064384 | tf_op jit(solution)/shard_map/attend/pallas_call | solution.py:182
  63.0 7.2 %collective-permute-start.9 = (f32[2,136,768]{2,1,0:T(8,128)S(1)}, f32[2,136,768]{2,1,0:T(8,128)S(1)}, u32[]{:S(2)}, u32[]{:S(2)}) collective-permute-start(f32[2,136,768]{2,1,0:T(8,128)S(1)} %attend.9), channel_id=1, source_target_pairs={{0,4},{4,0},{1,5},{5,1},{2,6},{6,2},{3,7},{7,3},{8,12},{12,8},{9,1... | collective-permute-start | bytes 2506760 | tf_op jit(solution)/shard_map/ppermute | solution.py:339
  70.1 2.0 %attend.8.mine = f32[2,136,768]{2,1,0:T(8,128)S(1)} custom-call(s32[4]{0:T(128)S(1)} %get-tuple-element.73.refs_0_, s32[4]{0:T(128)S(1)} %get-tuple-element.64.refs_1_, s32[4,24]{1,0:T(4,128)S(1)} %get-tuple-element.69.refs_2_, s32[4,24]{1,0:T(4,128)S(1)} %get-tuple-element.54.refs_3_, s32[4]{0:T(128)S(1)} %select_reduce_fusion.3.refs_4_, ...), custom_call_target="tpu_custom_call" | custom-call | flops 301989888 | bytes 2064384 | tf_op jit(solution)/shard_map/attend/pallas_call | solution.py:182
  72.2 0.0 collective-permute-done.9.theirs
  72.2 0.3 merge.1
  72.4 1.8 %collective-permute-start.10 = (bf16[48,1024]{1,0:T(8,128)(2,1)S(1)}, bf16[48,1024]{1,0:T(8,128)(2,1)S(1)}, u32[]{:S(2)}, u32[]{:S(2)}) collective-permute-start(bf16[48,1024]{1,0:T(8,128)(2,1)S(1)} %get-tuple-element.46), channel_id=1, source_target_pairs={{0,1},{1,2},{2,3},{3,0},{4,5},{5,6},{6,7},{7,4},{8,9},{9,10},{10,1... | collective-permute-start | bytes 294920 | tf_op jit(solution)/shard_map/ppermute | solution.py:343
  74.3 2.4 %collective-permute-start.11 = (bf16[48,1024]{1,0:T(8,128)(2,1)S(1)}, bf16[48,1024]{1,0:T(8,128)(2,1)S(1)}, u32[]{:S(2)}, u32[]{:S(2)}) collective-permute-start(bf16[48,1024]{1,0:T(8,128)(2,1)S(1)} %get-tuple-element.47), channel_id=1, source_target_pairs={{0,2},{1,3},{2,0},{3,1},{4,6},{5,7},{6,4},{7,5},{8,10},{9,11},{10,... | collective-permute-start | bytes 294920 | tf_op jit(solution)/shard_map/ppermute | solution.py:343
  76.6 1.2 %collective-permute-start.12 = (bf16[48,1024]{1,0:T(8,128)(2,1)S(1)}, bf16[48,1024]{1,0:T(8,128)(2,1)S(1)}, u32[]{:S(2)}, u32[]{:S(2)}) collective-permute-start(bf16[48,1024]{1,0:T(8,128)(2,1)S(1)} %get-tuple-element.48), channel_id=1, source_target_pairs={{0,3},{1,0},{2,1},{3,2},{4,7},{5,4},{6,5},{7,6},{8,11},{9,8},{10,9... | collective-permute-start | bytes 294920 | tf_op jit(solution)/shard_map/ppermute | solution.py:343
  77.8 0.5 collective-permute-done.10.refs_1_
  78.3 3.0 %collective-permute-done.11.refs_2_ = bf16[48,1024]{1,0:T(8,128)(2,1)S(1)} collective-permute-done((bf16[48,1024]{1,0:T(8,128)(2,1)S(1)}, bf16[48,1024]{1,0:T(8,128)(2,1)S(1)}, u32[]{:S(2)}, u32[]{:S(2)}) %collective-permute-start.11) | collective-permute-done | bytes 98336 | tf_op jit(solution)/shard_map/ppermute | solution.py:343
  81.3 0.0 collective-permute-done.12.refs_3_
  81.4 0.8 join.1
  (10 shorter events, 0.1 us)
Async XLA Ops:
  1.6 7.8 %copy-start.3 = (s32[4,24]{1,0:T(4,128)S(1)}, s32[4,24]{1,0:T(4,128)}, u32[]{:S(2)}) copy-start(s32[4,24]{1,0:T(4,128)} %constant.65.clone) | copy-start | bytes 1156
  1.7 9.9 %copy-start = (bf16[48,4096]{1,0:T(8,128)(2,1)S(1)}, bf16[48,4096]{1,0:T(8,128)(2,1)}, u32[]{:S(2)}) copy-start(bf16[48,4096]{1,0:T(8,128)(2,1)} %param.11) | copy-start | bytes 1179652
  1.7 16.0 %all-to-all-start.1 = ((bf16[16,48,256]{2,1,0:T(8,128)(2,1)}), bf16[16,48,256]{2,1,0:T(8,128)(2,1)S(1)}, u32[]{:S(2)}, u32[]{:S(2)}) async-start(bf16[16,48,256]{2,1,0:T(8,128)(2,1)} %spread.1), calls=%async_computation.1 | async-start | bytes 786432 | tf_op jit(solution)/shard_map/all_to_all | solution.py:305
  9.4 0.7 copy-start.2
  9.4 0.7 copy-start.1
  10.1 0.7 copy-start.7
  10.8 0.7 copy-start.8
  12.3 0.7 copy-start.4
  12.3 0.7 copy-start.5
  12.3 0.7 copy-start.6
  17.7 10.0 %all-to-all-start = ((bf16[48,4,1024]{2,0,1:T(8,128)(2,1)}), bf16[48,4,1024]{2,0,1:T(8,128)(2,1)S(1)}, u32[]{:S(2)}, u32[]{:S(2)}) async-start(bf16[48,4,1024]{2,0,1:T(8,128)(2,1)} %bitcast.40), calls=%async_computation | async-start | bytes 786432 | tf_op jit(solution)/shard_map/all_to_all | solution.py:308
  21.3 11.6 %collective-permute-start.2 = (bf16[768,256]{1,0:T(8,128)(2,1)S(1)}, bf16[768,256]{1,0:T(8,128)(2,1)S(1)}, u32[]{:S(2)}, u32[]{:S(2)}) collective-permute-start(bf16[768,256]{1,0:T(8,128)(2,1)S(1)} %bitcast.46), channel_id=1, source_target_pairs={{0,56},{8,0},{16,8},{24,16},{32,24},{40,32},{48,40},{56,48},{1,57}... | collective-permute-start | bytes 1179656 | tf_op jit(solution)/shard_map/ppermute | solution.py:325
  27.0 9.6 %collective-permute-start = (bf16[768,256]{1,0:T(8,128)(2,1)S(1)}, bf16[768,256]{1,0:T(8,128)(2,1)S(1)}, u32[]{:S(2)}, u32[]{:S(2)}) collective-permute-start(bf16[768,256]{1,0:T(8,128)(2,1)S(1)} %bitcast.47), channel_id=1, source_target_pairs={{0,8},{8,16},{16,24},{24,32},{32,40},{40,48},{48,56},{56,0},{1,9},... | collective-permute-start | bytes 1179656 | tf_op jit(solution)/shard_map/ppermute | solution.py:325
  27.7 8.9 %collective-permute-start.4 = (bf16[192,1024]{1,0:T(8,128)(2,1)S(1)}, bf16[192,1024]{1,0:T(8,128)(2,1)S(1)}, u32[]{:S(2)}, u32[]{:S(2)}) collective-permute-start(bf16[192,1024]{1,0:T(8,128)(2,1)S(1)} %bitcast.41), channel_id=1, source_target_pairs={{0,4},{4,0},{1,5},{5,1},{2,6},{6,2},{3,7},{7,3},{8,12},{12,8},{9,1... | collective-permute-start | bytes 1179656 | tf_op jit(solution)/shard_map/ppermute | solution.py:309
  33.0 11.8 %collective-permute-start.3 = (bf16[768,256]{1,0:T(8,128)(2,1)S(1)}, bf16[768,256]{1,0:T(8,128)(2,1)S(1)}, u32[]{:S(2)}, u32[]{:S(2)}) collective-permute-start(bf16[768,256]{1,0:T(8,128)(2,1)S(1)} %collective-permute-done.2.refs_9_), channel_id=1, source_target_pairs={{0,56},{8,0},{16,8},{24,16},{32,24},{40,32},{48,40},{56,48},{1,57}... | collective-permute-start | bytes 1179656 | tf_op jit(solution)/shard_map/ppermute | solution.py:329
  36.6 8.4 %collective-permute-start.1 = (bf16[768,256]{1,0:T(8,128)(2,1)S(1)}, bf16[768,256]{1,0:T(8,128)(2,1)S(1)}, u32[]{:S(2)}, u32[]{:S(2)}) collective-permute-start(bf16[768,256]{1,0:T(8,128)(2,1)S(1)} %collective-permute-done.refs_8_), channel_id=1, source_target_pairs={{0,8},{8,16},{16,24},{24,32},{32,40},{40,48},{48,56},{56,0},{1,9},... | collective-permute-start | bytes 1179656 | tf_op jit(solution)/shard_map/ppermute | solution.py:329
  45.0 7.8 %collective-permute-start.5 = (bf16[768,256]{1,0:T(8,128)(2,1)S(1)}, bf16[768,256]{1,0:T(8,128)(2,1)S(1)}, u32[]{:S(2)}, u32[]{:S(2)}) collective-permute-start(bf16[768,256]{1,0:T(8,128)(2,1)S(1)} %collective-permute-done.1.refs_7_), channel_id=1, source_target_pairs={{0,8},{8,16},{16,24},{24,32},{32,40},{40,48},{48,56},{56,0},{1,9},... | collective-permute-start | bytes 1179656 | tf_op jit(solution)/shard_map/ppermute | solution.py:329
  45.0 7.9 %collective-permute-start.6 = (bf16[768,256]{1,0:T(8,128)(2,1)S(1)}, bf16[768,256]{1,0:T(8,128)(2,1)S(1)}, u32[]{:S(2)}, u32[]{:S(2)}) collective-permute-start(bf16[768,256]{1,0:T(8,128)(2,1)S(1)} %collective-permute-done.3.refs_8_), channel_id=1, source_target_pairs={{0,56},{8,0},{16,8},{24,16},{32,24},{40,32},{48,40},{56,48},{1,57}... | collective-permute-start | bytes 1179656 | tf_op jit(solution)/shard_map/ppermute | solution.py:329
  52.9 8.0 %collective-permute-start.7 = (bf16[384,256]{1,0:T(8,128)(2,1)S(1)}, bf16[384,256]{1,0:T(8,128)(2,1)S(1)}, u32[]{:S(2)}, u32[]{:S(2)}) collective-permute-start(bf16[384,256]{1,0:T(8,128)(2,1)S(1)} %slice.66), channel_id=1, source_target_pairs={{0,8},{8,16},{16,24},{24,32},{32,40},{40,48},{48,56},{56,0},{1,9},... | collective-permute-start | bytes 589832 | tf_op jit(solution)/shard_map/ppermute | solution.py:332
  53.0 7.9 %collective-permute-start.8 = (bf16[384,256]{1,0:T(8,128)(2,1)S(1)}, bf16[384,256]{1,0:T(8,128)(2,1)S(1)}, u32[]{:S(2)}, u32[]{:S(2)}) collective-permute-start(bf16[384,256]{1,0:T(8,128)(2,1)S(1)} %slice.67), channel_id=1, source_target_pairs={{0,56},{8,0},{16,8},{24,16},{32,24},{40,32},{48,40},{56,48},{1,57}... | collective-permute-start | bytes 589832 | tf_op jit(solution)/shard_map/ppermute | solution.py:332
  63.0 9.2 %collective-permute-start.9 = (f32[2,136,768]{2,1,0:T(8,128)S(1)}, f32[2,136,768]{2,1,0:T(8,128)S(1)}, u32[]{:S(2)}, u32[]{:S(2)}) collective-permute-start(f32[2,136,768]{2,1,0:T(8,128)S(1)} %attend.9), channel_id=1, source_target_pairs={{0,4},{4,0},{1,5},{5,1},{2,6},{6,2},{3,7},{7,3},{8,12},{12,8},{9,1... | collective-permute-start | bytes 2506760 | tf_op jit(solution)/shard_map/ppermute | solution.py:339
  72.4 5.9 %collective-permute-start.10 = (bf16[48,1024]{1,0:T(8,128)(2,1)S(1)}, bf16[48,1024]{1,0:T(8,128)(2,1)S(1)}, u32[]{:S(2)}, u32[]{:S(2)}) collective-permute-start(bf16[48,1024]{1,0:T(8,128)(2,1)S(1)} %get-tuple-element.46), channel_id=1, source_target_pairs={{0,1},{1,2},{2,3},{3,0},{4,5},{5,6},{6,7},{7,4},{8,9},{9,10},{10,1... | collective-permute-start | bytes 294920 | tf_op jit(solution)/shard_map/ppermute | solution.py:343
  74.3 7.1 %collective-permute-start.11 = (bf16[48,1024]{1,0:T(8,128)(2,1)S(1)}, bf16[48,1024]{1,0:T(8,128)(2,1)S(1)}, u32[]{:S(2)}, u32[]{:S(2)}) collective-permute-start(bf16[48,1024]{1,0:T(8,128)(2,1)S(1)} %get-tuple-element.47), channel_id=1, source_target_pairs={{0,2},{1,3},{2,0},{3,1},{4,6},{5,7},{6,4},{7,5},{8,10},{9,11},{10,... | collective-permute-start | bytes 294920 | tf_op jit(solution)/shard_map/ppermute | solution.py:343
  76.6 4.7 %collective-permute-start.12 = (bf16[48,1024]{1,0:T(8,128)(2,1)S(1)}, bf16[48,1024]{1,0:T(8,128)(2,1)S(1)}, u32[]{:S(2)}, u32[]{:S(2)}) collective-permute-start(bf16[48,1024]{1,0:T(8,128)(2,1)S(1)} %get-tuple-element.48), channel_id=1, source_target_pairs={{0,3},{1,0},{2,1},{3,2},{4,7},{5,4},{6,5},{7,6},{8,11},{9,8},{10,9... | collective-permute-start | bytes 294920 | tf_op jit(solution)/shard_map/ppermute | solution.py:343

commit v3 on v2

--- a/solution.py
+++ b/solution.py
@@ -305,15 +305,12 @@
     line = lax.all_to_all(spread(keys, values), ("x", "tp"), split_axis=0, concat_axis=0, tiled=True)
     line = line.reshape(-1, 2 * HEAD)
 
-    q_own = lax.all_to_all(queries, "tp", split_axis=1, concat_axis=0, tiled=True)
-    q_other = lax.ppermute(q_own, "c", shift(2, 1))
-
     ctx = (x * NZ + z) * 2
     own = np.asarray([1, 1, 0, 0], np.int32)
     core = own * c + (1 - own) * (1 - c)
     qpos = lookup(block_order, 2 * (ctx + core) + np.asarray([0, 1, 0, 1], np.int32))
 
-    offsets = [(0, -1, 1), (-2, 2), (-3, 3), (NZ // 2,)]
+    offsets = [(0, -1), (1, -2, 2), (-3, 3), (NZ // 2,)]
     most = 2 * NX * max(len(o) for o in offsets)
     dz, dx, slot, real = (np.zeros((len(offsets), most), np.int32) for _ in range(4))
     for i, group in enumerate(offsets):
@@ -321,9 +318,14 @@
             dz[i, j], dx[i, j], slot[i, j], real[i, j] = o, xs, sl, 1
     stored = lookup(block_order, (2 * ((dx * NZ + (z + dz) % NZ) * 2 + c) + slot).reshape(-1)).reshape(dz.shape)
     tables = tables_of(qpos, jnp.where(real == 1, stored, 1 << 20))
+    queries, *tables = lax.optimization_barrier((queries, *tables))
+
+    q_own = lax.all_to_all(queries, "tp", split_axis=1, concat_axis=0, tiled=True)
+    q_other = lax.ppermute(q_own, "c", shift(2, 1))
 
     up, down = lax.ppermute(line, "z", shift(NZ, 1)), lax.ppermute(line, "z", shift(NZ, -1))
-    pieces, state = [line, up, down], None
+    pieces, state = [line, up], None
+    later = [down]
     for i in range(len(offsets)):
         if i < len(offsets) - 2:
             up, down = lax.ppermute(up, "z", shift(NZ, 1)), lax.ppermute(down, "z", shift(NZ, -1))
@@ -334,7 +336,7 @@
         if i < len(offsets) - 1:
             state = attend(part, qpos, (q_own, q_other), pieces, state)
             up, down, state = lax.optimization_barrier((up, down, state))
-            pieces = [up, down]
+            pieces, later = later + [up, down], []
     (sent,) = attend(part, qpos, (q_own, q_other), pieces, state, (1,))
     theirs = lax.ppermute(sent, "c", shift(2, 1))
     (mine,) = attend(part, qpos, (q_own, q_other), pieces, state, (0,))

time: 82.5 us -> 86 us (1.042)
  starting transfers between devices: 42.1 us -> 31.2 us
  blocking collectives: 0 us -> 8.92 us
  waiting for transfers between devices: 10.3 us -> 15.9 us
    all_to_all x0 -> x1, blocking collectives: none -> 8.92 us  [attention(): lax.all_to_all(queries, 'tp', split_axis=1, concat_axis=0, tiled=True)]
    ppermute x2, waiting for transfers between devices: 0.28 us -> 4.7 us  [attention(): lax.ppermute(up, 'z', shift(NZ, 1))]
    ppermute x1, starting transfers between devices: 7.15 us -> 2.86 us  [attention(): theirs = lax.ppermute(sent, 'c', shift(2, 1))]
    all_to_all x1 -> x0, starting transfers between devices: 3.46 us -> none  [attention(): lax.all_to_all(queries, 'tp', split_axis=1, concat_axis=0, tiled=True)]
    ppermute x3, starting transfers between devices: 5.38 us -> 2.86 us  [attention(): lax.ppermute(parts[k], 'tp', shift(4, k))]
    ppermute x1, waiting for transfers between devices: 1.97 us -> 0.01 us  [attention(): lax.ppermute(line, 'z', shift(NZ, -1))]
    ppermute x2, waiting for transfers between devices: 0.01 us -> 1.77 us  [attention(): lax.ppermute(down, 'z', shift(NZ, -1))]
    ppermute x3, waiting for transfers between devices: 3.52 us -> 5 us  [attention(): lax.ppermute(parts[k], 'tp', shift(4, k))]
  transfers between devices with their start and end apart: 15 -> 14, of which waited for: 5 -> 7; matrix products, arithmetic and copies ran while one was open for 3% -> 2% of each run, Pallas kernels for 24% -> 24%
where the time goes in v3:
time: 86 us; the launch traced here: 85.2 us
  starting transfers between devices  31.2 us (36%)
  Pallas kernels  24.9 us (29%)
  waiting for transfers between devices  15.9 us (18%)
  blocking collectives  8.92 us (10%)
  local copies, waits for them, and re-layouts  2.74 us (3%)
  other arithmetic  1.27 us (1%)
    pallas_call x5, Pallas kernels, attend(): pl.pallas_call(functools.partial(attend_kernel, counts, first, sides), ou...  22.3 us
    all_to_all x1, blocking collectives, attention(): lax.all_to_all(queries, 'tp', split_axis=1, concat_axis=0, tiled=True)  8.92 us
    all_to_all x1, starting transfers between devices, attention(): lax.all_to_all(spread(keys, values), ('x', 'tp'), split_axis=0, concat_ax...  7.72 us
    ppermute x2, starting transfers between devices, attention(): lax.ppermute(down, 'z', shift(NZ, -1))  5.63 us
    ppermute x1, starting transfers between devices, attention(): lax.ppermute(line, 'z', shift(NZ, -1))  5.58 us
    ppermute x3, waiting for transfers between devices, attention(): lax.ppermute(parts[k], 'tp', shift(4, k))  5 us
    ppermute x2, waiting for transfers between devices, attention(): lax.ppermute(up, 'z', shift(NZ, 1))  4.7 us
    all_to_all x1, waiting for transfers between devices, attention(): lax.all_to_all(spread(keys, values), ('x', 'tp'), split_axis=0, concat_ax...  4.45 us
  transfers between devices with their start and end apart: 14, of which 7 were waited for; matrix products, arithmetic and copies ran while one was open for 2% of the time, Pallas kernels for 24%

profile of v3, /device:TPU:1, one launch (start us, length us, event | category | flops | bytes accessed | tf_op | source)
XLA Modules:
  0.0 85.2 jit_solution(7647581102347966594)
XLA Ops:
  0.0 1.6 %spread.1 = bf16[16,48,256]{2,1,0:T(8,128)(2,1)} custom-call(bf16[48,512]{1,0:T(8,128)(2,1)} %keys.1, bf16[48,512]{1,0:T(8,128)(2,1)} %values.1), custom_call_target="tpu_custom_call" | custom-call | tf_op jit(solution)/shard_map/spread/pallas_call | solution.py:282
  1.6 0.0 copy-start
  1.7 7.7 %all-to-all-start.1 = ((bf16[16,48,256]{2,1,0:T(8,128)(2,1)}), bf16[16,48,256]{2,1,0:T(8,128)(2,1)S(1)}, u32[]{:S(2)}, u32[]{:S(2)}) async-start(bf16[16,48,256]{2,1,0:T(8,128)(2,1)} %spread.1), calls=%async_computation.1 | async-start | bytes 786432 | tf_op jit(solution)/shard_map/all_to_all | solution.py:305
  9.4 0.0 copy-start.3
  9.4 0.0 copy-start.2
  9.4 0.0 copy-start.1
  9.4 0.6 copy-done.3
  10.1 0.0 copy-done.2
  10.1 0.0 copy-done.1
  10.1 0.1 eq.60
  10.2 0.0 copy-start.4
  10.2 0.0 copy-start.5
  10.2 0.0 copy-start.6
  10.2 0.6 copy-done.4
  10.9 0.0 copy-done.5
  10.9 0.0 copy-done.6
  10.9 0.0 copy-start.7
  10.9 0.6 copy-done.7
  11.5 0.2 select_reduce_fusion.3.refs_4_
  11.7 0.0 copy-start.8
  11.7 0.2 select_reduce_fusion.2
  11.9 0.5 copy-done.8
  12.4 0.1 reshape.38
  12.5 0.2 compare_select_fusion
  12.7 0.5 convert_reduce_fusion
  13.2 4.4 %all-to-all-done.1 = bf16[16,48,256]{2,1,0:T(8,128)(2,1)S(1)} async-done(((bf16[16,48,256]{2,1,0:T(8,128)(2,1)}), bf16[16,48,256]{2,1,0:T(8,128)(2,1)S(1)}, u32[]{:S(2)}, u32[]{:S(2)}) %all-to-all-start.1) | async-done | bytes 393248 | tf_op jit(solution)/shard_map/all_to_all | solution.py:305
  17.6 5.6 %collective-permute-start.2 = (bf16[768,256]{1,0:T(8,128)(2,1)S(1)}, bf16[768,256]{1,0:T(8,128)(2,1)S(1)}, u32[]{:S(2)}, u32[]{:S(2)}) collective-permute-start(bf16[768,256]{1,0:T(8,128)(2,1)S(1)} %bitcast.46), channel_id=1, source_target_pairs={{0,56},{8,0},{16,8},{24,16},{32,24},{40,32},{48,40},{56,48},{1,57}... | collective-permute-start | bytes 1179656 | tf_op jit(solution)/shard_map/ppermute | solution.py:326
  23.2 0.0 collective-permute-start
  23.2 0.2 select_reduce_fusion
  23.4 0.0 copy-done
  23.4 8.9 %all_to_all.24 = bf16[48,4,1024]{2,0,1:T(8,128)(2,1)S(1)} all-to-all(bf16[48,4,1024]{2,0,1:T(8,128)(2,1)S(1)} %bitcast.49), channel_id=1, replica_groups=mesh['x'=4,'z'=8,'c'=2,'tp'=4] {'tp'}, dimensions={1} | all-to-all | bytes 786432 | tf_op jit(solution)/shard_map/all_to_all | solution.py:323
  32.4 3.8 %collective-permute-start.4 = (bf16[192,1024]{1,0:T(8,128)(2,1)S(1)}, bf16[192,1024]{1,0:T(8,128)(2,1)S(1)}, u32[]{:S(2)}, u32[]{:S(2)}) collective-permute-start(bf16[192,1024]{1,0:T(8,128)(2,1)S(1)} %bitcast.41), channel_id=1, source_target_pairs={{0,4},{4,0},{1,5},{5,1},{2,6},{6,2},{3,7},{7,3},{8,12},{12,8},{9,1... | collective-permute-start | bytes 1179656 | tf_op jit(solution)/shard_map/ppermute | solution.py:324
  36.1 0.0 collective-permute-done.2.refs_7_
  36.1 3.0 %collective-permute-start.3 = (bf16[768,256]{1,0:T(8,128)(2,1)S(1)}, bf16[768,256]{1,0:T(8,128)(2,1)S(1)}, u32[]{:S(2)}, u32[]{:S(2)}) collective-permute-start(bf16[768,256]{1,0:T(8,128)(2,1)S(1)} %collective-permute-done.2.refs_7_), channel_id=1, source_target_pairs={{0,56},{8,0},{16,8},{24,16},{32,24},{40,32},{48,40},{56,48},{1,57}... | collective-permute-start | bytes 1179656 | tf_op jit(solution)/shard_map/ppermute | solution.py:331
  39.1 0.0 collective-permute-done.refs_8_
  39.1 0.0 collective-permute-start.1
  39.1 0.0 collective-permute-done.4.refs_6_.refs_5_
  39.1 6.7 %attend.5 = (f32[2,136,768]{2,1,0:T(8,128)S(1)}, f32[2,136,768]{2,1,0:T(8,128)S(1)}) custom-call(s32[4]{0:T(128)S(1)} %get-tuple-element.84.refs_0_, s32[4]{0:T(128)S(1)} %get-tuple-element.73.refs_1_, s32[4,24]{1,0:T(4,128)S(1)} %get-tuple-element.80.refs_2_, s32[4,24]{1,0:T(4,128)S(1)} %get-tuple-element.63.refs_3_, s32[4]{0:T(128)S(1)} %select_reduce_fusion.3.refs_4_, ...), custom_call_target="tpu_custom_call" | custom-call | flops 1207959552 | bytes 2457600 | tf_op jit(solution)/shard_map/attend/pallas_call | solution.py:182
  45.8 1.8 %collective-permute-done.3.refs_9_ = bf16[768,256]{1,0:T(8,128)(2,1)S(1)} collective-permute-done((bf16[768,256]{1,0:T(8,128)(2,1)S(1)}, bf16[768,256]{1,0:T(8,128)(2,1)S(1)}, u32[]{:S(2)}, u32[]{:S(2)}) %collective-permute-start.3) | collective-permute-done | bytes 393248 | tf_op jit(solution)/shard_map/ppermute | solution.py:331
  47.6 3.1 %collective-permute-done.1.refs_8_ = bf16[768,256]{1,0:T(8,128)(2,1)S(1)} collective-permute-done((bf16[768,256]{1,0:T(8,128)(2,1)S(1)}, bf16[768,256]{1,0:T(8,128)(2,1)S(1)}, u32[]{:S(2)}, u32[]{:S(2)}) %collective-permute-start.1) | collective-permute-done | bytes 393248 | tf_op jit(solution)/shard_map/ppermute | solution.py:331
  50.7 0.0 collective-permute-start.5
  50.7 2.7 %collective-permute-start.6 = (bf16[768,256]{1,0:T(8,128)(2,1)S(1)}, bf16[768,256]{1,0:T(8,128)(2,1)S(1)}, u32[]{:S(2)}, u32[]{:S(2)}) collective-permute-start(bf16[768,256]{1,0:T(8,128)(2,1)S(1)} %collective-permute-done.3.refs_9_), channel_id=1, source_target_pairs={{0,56},{8,0},{16,8},{24,16},{32,24},{40,32},{48,40},{56,48},{1,57}... | collective-permute-start | bytes 1179656 | tf_op jit(solution)/shard_map/ppermute | solution.py:331
  53.4 6.5 %attend.6 = (f32[2,136,768]{2,1,0:T(8,128)S(1)}, f32[2,136,768]{2,1,0:T(8,128)S(1)}) custom-call(s32[4]{0:T(128)S(1)} %get-tuple-element.85.refs_0_, s32[4]{0:T(128)S(1)} %get-tuple-element.72.refs_1_, s32[4,24]{1,0:T(4,128)S(1)} %get-tuple-element.81.refs_2_, s32[4,24]{1,0:T(4,128)S(1)} %get-tuple-element.62.refs_3_, s32[4]{0:T(128)S(1)} %select_reduce_fusion.3.refs_4_, ...), custom_call_target="tpu_custom_call" | custom-call | flops 1811939328 | bytes 2850816 | tf_op jit(solution)/shard_map/attend/pallas_call | solution.py:182
  59.9 1.6 %collective-permute-done.5.refs_7_ = bf16[768,256]{1,0:T(8,128)(2,1)S(1)} collective-permute-done((bf16[768,256]{1,0:T(8,128)(2,1)S(1)}, bf16[768,256]{1,0:T(8,128)(2,1)S(1)}, u32[]{:S(2)}, u32[]{:S(2)}) %collective-permute-start.5) | collective-permute-done | bytes 393248 | tf_op jit(solution)/shard_map/ppermute | solution.py:331
  61.4 0.0 collective-permute-done.6.refs_8_
  61.5 0.1 collective-permute-start.7
  61.6 2.7 %collective-permute-start.8 = (bf16[384,256]{1,0:T(8,128)(2,1)S(1)}, bf16[384,256]{1,0:T(8,128)(2,1)S(1)}, u32[]{:S(2)}, u32[]{:S(2)}) collective-permute-start(bf16[384,256]{1,0:T(8,128)(2,1)S(1)} %slice.67), channel_id=1, source_target_pairs={{0,56},{8,0},{16,8},{24,16},{32,24},{40,32},{48,40},{56,48},{1,57}... | collective-permute-start | bytes 589832 | tf_op jit(solution)/shard_map/ppermute | solution.py:334
  64.2 5.0 %attend.7 = (f32[2,136,768]{2,1,0:T(8,128)S(1)}, f32[2,136,768]{2,1,0:T(8,128)S(1)}) custom-call(s32[4]{0:T(128)S(1)} %get-tuple-element.86.refs_0_, s32[4]{0:T(128)S(1)} %get-tuple-element.71.refs_1_, s32[4,24]{1,0:T(4,128)S(1)} %get-tuple-element.82.refs_2_, s32[4,24]{1,0:T(4,128)S(1)} %get-tuple-element.61.refs_3_, s32[4]{0:T(128)S(1)} %select_reduce_fusion.3.refs_4_, ...), custom_call_target="tpu_custom_call" | custom-call | flops 1207959552 | bytes 2457600 | tf_op jit(solution)/shard_map/attend/pallas_call | solution.py:182
  69.3 0.0 collective-permute-done.7.refs_6_
  69.3 0.0 collective-permute-done.8.refs_7_
  69.3 2.0 %attend.9 = f32[2,136,768]{2,1,0:T(8,128)S(1)} custom-call(s32[4]{0:T(128)S(1)} %get-tuple-element.83.refs_0_, s32[4]{0:T(128)S(1)} %get-tuple-element.74.refs_1_, s32[4,24]{1,0:T(4,128)S(1)} %get-tuple-element.79.refs_2_, s32[4,24]{1,0:T(4,128)S(1)} %get-tuple-element.64.refs_3_, s32[4]{0:T(128)S(1)} %select_reduce_fusion.3.refs_4_, ...), custom_call_target="tpu_custom_call" | custom-call | flops 301989888 | bytes 2064384 | tf_op jit(solution)/shard_map/attend/pallas_call | solution.py:182
  71.3 2.9 %collective-permute-start.9 = (f32[2,136,768]{2,1,0:T(8,128)S(1)}, f32[2,136,768]{2,1,0:T(8,128)S(1)}, u32[]{:S(2)}, u32[]{:S(2)}) collective-permute-start(f32[2,136,768]{2,1,0:T(8,128)S(1)} %attend.9), channel_id=1, source_target_pairs={{0,4},{4,0},{1,5},{5,1},{2,6},{6,2},{3,7},{7,3},{8,12},{12,8},{9,1... | collective-permute-start | bytes 2506760 | tf_op jit(solution)/shard_map/ppermute | solution.py:341
  74.2 2.1 %attend.8.mine = f32[2,136,768]{2,1,0:T(8,128)S(1)} custom-call(s32[4]{0:T(128)S(1)} %get-tuple-element.83.refs_0_, s32[4]{0:T(128)S(1)} %get-tuple-element.74.refs_1_, s32[4,24]{1,0:T(4,128)S(1)} %get-tuple-element.79.refs_2_, s32[4,24]{1,0:T(4,128)S(1)} %get-tuple-element.64.refs_3_, s32[4]{0:T(128)S(1)} %select_reduce_fusion.3.refs_4_, ...), custom_call_target="tpu_custom_call" | custom-call | flops 301989888 | bytes 2064384 | tf_op jit(solution)/shard_map/attend/pallas_call | solution.py:182
  76.3 0.0 collective-permute-done.9.theirs
  76.3 0.3 merge.1
  76.5 0.4 collective-permute-start.10
  76.9 1.8 %collective-permute-start.11 = (bf16[48,1024]{1,0:T(8,128)(2,1)S(1)}, bf16[48,1024]{1,0:T(8,128)(2,1)S(1)}, u32[]{:S(2)}, u32[]{:S(2)}) collective-permute-start(bf16[48,1024]{1,0:T(8,128)(2,1)S(1)} %get-tuple-element.57), channel_id=1, source_target_pairs={{0,2},{1,3},{2,0},{3,1},{4,6},{5,7},{6,4},{7,5},{8,10},{9,11},{10,... | collective-permute-start | bytes 294920 | tf_op jit(solution)/shard_map/ppermute | solution.py:345
  78.7 0.7 collective-permute-start.12
  79.4 3.1 %collective-permute-done.10.refs_1_ = bf16[48,1024]{1,0:T(8,128)(2,1)S(1)} collective-permute-done((bf16[48,1024]{1,0:T(8,128)(2,1)S(1)}, bf16[48,1024]{1,0:T(8,128)(2,1)S(1)}, u32[]{:S(2)}, u32[]{:S(2)}) %collective-permute-start.10) | collective-permute-done | bytes 98336 | tf_op jit(solution)/shard_map/ppermute | solution.py:345
  82.5 0.9 %collective-permute-done.11.refs_2_ = bf16[48,1024]{1,0:T(8,128)(2,1)S(1)} collective-permute-done((bf16[48,1024]{1,0:T(8,128)(2,1)S(1)}, bf16[48,1024]{1,0:T(8,128)(2,1)S(1)}, u32[]{:S(2)}, u32[]{:S(2)}) %collective-permute-start.11) | collective-permute-done | bytes 98336 | tf_op jit(solution)/shard_map/ppermute | solution.py:345
  83.4 1.0 %collective-permute-done.12.refs_3_ = bf16[48,1024]{1,0:T(8,128)(2,1)S(1)} collective-permute-done((bf16[48,1024]{1,0:T(8,128)(2,1)S(1)}, bf16[48,1024]{1,0:T(8,128)(2,1)S(1)}, u32[]{:S(2)}, u32[]{:S(2)}) %collective-permute-start.12) | collective-permute-done | bytes 98336 | tf_op jit(solution)/shard_map/ppermute | solution.py:345
  84.4 0.8 join.1
  (11 shorter events, 0.1 us)
Async XLA Ops:
  1.6 21.8 %copy-start = (bf16[48,4096]{1,0:T(8,128)(2,1)S(1)}, bf16[48,4096]{1,0:T(8,128)(2,1)}, u32[]{:S(2)}) copy-start(bf16[48,4096]{1,0:T(8,128)(2,1)} %param.11) | copy-start | bytes 1179652
  1.7 16.0 %all-to-all-start.1 = ((bf16[16,48,256]{2,1,0:T(8,128)(2,1)}), bf16[16,48,256]{2,1,0:T(8,128)(2,1)S(1)}, u32[]{:S(2)}, u32[]{:S(2)}) async-start(bf16[16,48,256]{2,1,0:T(8,128)(2,1)} %spread.1), calls=%async_computation.1 | async-start | bytes 786432 | tf_op jit(solution)/shard_map/all_to_all | solution.py:305
  9.4 0.7 copy-start.3
  9.4 0.7 copy-start.2
  9.4 0.7 copy-start.1
  10.2 0.7 copy-start.4
  10.2 0.7 copy-start.5
  10.2 0.7 copy-start.6
  10.9 0.7 copy-start.7
  11.7 0.7 copy-start.8
  17.6 18.5 %collective-permute-start.2 = (bf16[768,256]{1,0:T(8,128)(2,1)S(1)}, bf16[768,256]{1,0:T(8,128)(2,1)S(1)}, u32[]{:S(2)}, u32[]{:S(2)}) collective-permute-start(bf16[768,256]{1,0:T(8,128)(2,1)S(1)} %bitcast.46), channel_id=1, source_target_pairs={{0,56},{8,0},{16,8},{24,16},{32,24},{40,32},{48,40},{56,48},{1,57}... | collective-permute-start | bytes 1179656 | tf_op jit(solution)/shard_map/ppermute | solution.py:326
  23.2 15.9 %collective-permute-start = (bf16[768,256]{1,0:T(8,128)(2,1)S(1)}, bf16[768,256]{1,0:T(8,128)(2,1)S(1)}, u32[]{:S(2)}, u32[]{:S(2)}) collective-permute-start(bf16[768,256]{1,0:T(8,128)(2,1)S(1)} %bitcast.47), channel_id=1, source_target_pairs={{0,8},{8,16},{16,24},{24,32},{32,40},{40,48},{48,56},{56,0},{1,9},... | collective-permute-start | bytes 1179656 | tf_op jit(solution)/shard_map/ppermute | solution.py:326
  32.4 6.8 %collective-permute-start.4 = (bf16[192,1024]{1,0:T(8,128)(2,1)S(1)}, bf16[192,1024]{1,0:T(8,128)(2,1)S(1)}, u32[]{:S(2)}, u32[]{:S(2)}) collective-permute-start(bf16[192,1024]{1,0:T(8,128)(2,1)S(1)} %bitcast.41), channel_id=1, source_target_pairs={{0,4},{4,0},{1,5},{5,1},{2,6},{6,2},{3,7},{7,3},{8,12},{12,8},{9,1... | collective-permute-start | bytes 1179656 | tf_op jit(solution)/shard_map/ppermute | solution.py:324
  36.1 11.4 %collective-permute-start.3 = (bf16[768,256]{1,0:T(8,128)(2,1)S(1)}, bf16[768,256]{1,0:T(8,128)(2,1)S(1)}, u32[]{:S(2)}, u32[]{:S(2)}) collective-permute-start(bf16[768,256]{1,0:T(8,128)(2,1)S(1)} %collective-permute-done.2.refs_7_), channel_id=1, source_target_pairs={{0,56},{8,0},{16,8},{24,16},{32,24},{40,32},{48,40},{56,48},{1,57}... | collective-permute-start | bytes 1179656 | tf_op jit(solution)/shard_map/ppermute | solution.py:331
  39.1 11.6 %collective-permute-start.1 = (bf16[768,256]{1,0:T(8,128)(2,1)S(1)}, bf16[768,256]{1,0:T(8,128)(2,1)S(1)}, u32[]{:S(2)}, u32[]{:S(2)}) collective-permute-start(bf16[768,256]{1,0:T(8,128)(2,1)S(1)} %collective-permute-done.refs_8_), channel_id=1, source_target_pairs={{0,8},{8,16},{16,24},{24,32},{32,40},{40,48},{48,56},{56,0},{1,9},... | collective-permute-start | bytes 1179656 | tf_op jit(solution)/shard_map/ppermute | solution.py:331
  50.7 10.7 %collective-permute-start.5 = (bf16[768,256]{1,0:T(8,128)(2,1)S(1)}, bf16[768,256]{1,0:T(8,128)(2,1)S(1)}, u32[]{:S(2)}, u32[]{:S(2)}) collective-permute-start(bf16[768,256]{1,0:T(8,128)(2,1)S(1)} %collective-permute-done.1.refs_8_), channel_id=1, source_target_pairs={{0,8},{8,16},{16,24},{24,32},{32,40},{40,48},{48,56},{56,0},{1,9},... | collective-permute-start | bytes 1179656 | tf_op jit(solution)/shard_map/ppermute | solution.py:331
  50.7 10.7 %collective-permute-start.6 = (bf16[768,256]{1,0:T(8,128)(2,1)S(1)}, bf16[768,256]{1,0:T(8,128)(2,1)S(1)}, u32[]{:S(2)}, u32[]{:S(2)}) collective-permute-start(bf16[768,256]{1,0:T(8,128)(2,1)S(1)} %collective-permute-done.3.refs_9_), channel_id=1, source_target_pairs={{0,56},{8,0},{16,8},{24,16},{32,24},{40,32},{48,40},{56,48},{1,57}... | collective-permute-start | bytes 1179656 | tf_op jit(solution)/shard_map/ppermute | solution.py:331
  61.5 7.8 %collective-permute-start.7 = (bf16[384,256]{1,0:T(8,128)(2,1)S(1)}, bf16[384,256]{1,0:T(8,128)(2,1)S(1)}, u32[]{:S(2)}, u32[]{:S(2)}) collective-permute-start(bf16[384,256]{1,0:T(8,128)(2,1)S(1)} %slice.66), channel_id=1, source_target_pairs={{0,8},{8,16},{16,24},{24,32},{32,40},{40,48},{48,56},{56,0},{1,9},... | collective-permute-start | bytes 589832 | tf_op jit(solution)/shard_map/ppermute | solution.py:334
  61.6 7.7 %collective-permute-start.8 = (bf16[384,256]{1,0:T(8,128)(2,1)S(1)}, bf16[384,256]{1,0:T(8,128)(2,1)S(1)}, u32[]{:S(2)}, u32[]{:S(2)}) collective-permute-start(bf16[384,256]{1,0:T(8,128)(2,1)S(1)} %slice.67), channel_id=1, source_target_pairs={{0,56},{8,0},{16,8},{24,16},{32,24},{40,32},{48,40},{56,48},{1,57}... | collective-permute-start | bytes 589832 | tf_op jit(solution)/shard_map/ppermute | solution.py:334
  71.3 4.9 %collective-permute-start.9 = (f32[2,136,768]{2,1,0:T(8,128)S(1)}, f32[2,136,768]{2,1,0:T(8,128)S(1)}, u32[]{:S(2)}, u32[]{:S(2)}) collective-permute-start(f32[2,136,768]{2,1,0:T(8,128)S(1)} %attend.9), channel_id=1, source_target_pairs={{0,4},{4,0},{1,5},{5,1},{2,6},{6,2},{3,7},{7,3},{8,12},{12,8},{9,1... | collective-permute-start | bytes 2506760 | tf_op jit(solution)/shard_map/ppermute | solution.py:341
  76.5 5.9 %collective-permute-start.10 = (bf16[48,1024]{1,0:T(8,128)(2,1)S(1)}, bf16[48,1024]{1,0:T(8,128)(2,1)S(1)}, u32[]{:S(2)}, u32[]{:S(2)}) collective-permute-start(bf16[48,1024]{1,0:T(8,128)(2,1)S(1)} %get-tuple-element.56), channel_id=1, source_target_pairs={{0,1},{1,2},{2,3},{3,0},{4,5},{5,6},{6,7},{7,4},{8,9},{9,10},{10,1... | collective-permute-start | bytes 294920 | tf_op jit(solution)/shard_map/ppermute | solution.py:345
  76.9 6.5 %collective-permute-start.11 = (bf16[48,1024]{1,0:T(8,128)(2,1)S(1)}, bf16[48,1024]{1,0:T(8,128)(2,1)S(1)}, u32[]{:S(2)}, u32[]{:S(2)}) collective-permute-start(bf16[48,1024]{1,0:T(8,128)(2,1)S(1)} %get-tuple-element.57), channel_id=1, source_target_pairs={{0,2},{1,3},{2,0},{3,1},{4,6},{5,7},{6,4},{7,5},{8,10},{9,11},{10,... | collective-permute-start | bytes 294920 | tf_op jit(solution)/shard_map/ppermute | solution.py:345
  78.7 5.7 %collective-permute-start.12 = (bf16[48,1024]{1,0:T(8,128)(2,1)S(1)}, bf16[48,1024]{1,0:T(8,128)(2,1)S(1)}, u32[]{:S(2)}, u32[]{:S(2)}) collective-permute-start(bf16[48,1024]{1,0:T(8,128)(2,1)S(1)} %get-tuple-element.58), channel_id=1, source_target_pairs={{0,3},{1,0},{2,1},{3,2},{4,7},{5,4},{6,5},{7,6},{8,11},{9,8},{10,9... | collective-permute-start | bytes 294920 | tf_op jit(solution)/shard_map/ppermute | solution.py:345
